TPU v7x, 32 devices: a whole 2x2x4 slice. The times are simulated.
32 devices in a mesh: dp: 2 (over core), seq: 8 (over z, x), mp: 2 (over y).
Axes of the slice: x: 2, y: 2, z: 4, core: 2. Of those that a mesh axis runs over, the one named last changes fastest.
Arguments:
- queries: bfloat16 [4, 1024, 4096], P('dp', 'seq', 'mp'), may hold values from -6 to 6
- vision: bfloat16 [4, 640, 4096], P('dp', 'seq'), may hold values from -6 to 6
- key_weight: bfloat16 [4096, 1024], P(None, 'mp'), may hold values from -0.09375 to 0.09375
- value_weight: bfloat16 [4096, 1024], P(None, 'mp'), may hold values from -0.09375 to 0.09375
- query_gain: float32 [128], replicated, may hold values from 0.6 to 6
- key_gain: float32 [128], replicated, may hold values from 0.6 to 6
- out_grad: bfloat16 [4, 1024, 4096], P('dp', 'seq', 'mp'), may hold values from -6 to 6
- tile_count: int32 [4], P('dp'), may hold values from 1 to 4, as said below
Outputs:
- query_grad: bfloat16 [4, 1024, 4096], P('dp', 'seq', 'mp')
- vision_grad: bfloat16 [4, 640, 4096], P('dp', 'seq', 'mp')
- key_weight_grad: float32 [4096, 1024], P(None, 'mp')
- value_weight_grad: float32 [4096, 1024], P(None, 'mp')
Inputs may be any that keep to these rules, and one draw needn't show every extreme that they name: The live vision tokens of sample s are its first tile_count[s] * 160; some sample has 4 tiles and some other sample has 1.
All inputs are finite; a program needn't handle non-finite values.
Results may differ from a plain program's by a relative error of at most 0.03.
The roundings to bfloat16 on the way count: a program that leaves them out, or rounds other values in their place, can miss the bound.
Values may be sent and summed in bfloat16 or wider, within the bound.
A program may use at most 128 MiB of HBM per device.

v0:
```python
import jax
import jax.numpy as jnp
from jax import lax
from jax.sharding import PartitionSpec as P

MAX_TILES = 4


EPS = 1e-05
NEG = -1e30


def norm_apply(raw, gain):
    inverse = lax.rsqrt(jnp.mean(raw * raw, axis=-1, keepdims=True) + EPS)
    return (raw * inverse * gain, inverse)


def norm_back(raw, inverse, gain, upstream):
    weighted = upstream * gain
    return inverse * weighted - raw * inverse * inverse * inverse * jnp.mean(
        weighted * raw, axis=-1, keepdims=True
    )


def sample_grads(normed, out_heads, keys_all, values_all, tiles_here, score_scale):
    text_rows, kv_here, group_size, head_dim = normed.shape
    block_len = keys_all.shape[0] // MAX_TILES
    stat_shape = (kv_here, group_size, text_rows, 1)

    def scores_of(block_at):
        key_block = keys_all[block_at * block_len : (block_at + 1) * block_len]
        return (
            jnp.einsum("tkgd,jkd->kgtj", normed, key_block, preferred_element_type=jnp.float32)
            * score_scale
        )

    row_max = jnp.full(stat_shape, NEG, jnp.float32)
    row_sum = jnp.zeros(stat_shape, jnp.float32)
    for block_at in range(MAX_TILES):
        live_flag = block_at < tiles_here

        def update_stats(carry, block_at=block_at, live_flag=live_flag):
            old_max, old_sum = carry
            scores = jnp.where(live_flag, scores_of(block_at), NEG)
            new_max = jnp.maximum(old_max, jnp.max(scores, axis=-1, keepdims=True))
            new_sum = old_sum * jnp.exp(old_max - new_max) + jnp.sum(
                jnp.exp(scores - new_max), axis=-1, keepdims=True
            )
            return (new_max, new_sum)

        row_max, row_sum = update_stats((row_max, row_sum))

    def probs_of(block_at, live_flag):
        scores = scores_of(block_at)
        return jnp.where(live_flag, jnp.exp(scores - row_max) / row_sum, 0.0)

    attn_total = jnp.zeros((text_rows, kv_here, group_size, head_dim), jnp.float32)
    value_part = jnp.zeros((keys_all.shape[0], kv_here, head_dim), jnp.float32)
    for block_at in range(MAX_TILES):
        live_flag = block_at < tiles_here

        def forward_block(carry, block_at=block_at, live_flag=live_flag):
            attn_now, value_now = carry
            probs_b = probs_of(block_at, live_flag).astype(jnp.bfloat16)
            value_block = values_all[block_at * block_len : (block_at + 1) * block_len]
            attn_now = attn_now + jnp.einsum(
                "kgtj,jkd->tkgd", probs_b, value_block, preferred_element_type=jnp.float32
            )
            block_grad = jnp.einsum(
                "kgtj,tkgd->jkd", probs_b, out_heads, preferred_element_type=jnp.float32
            )
            value_now = value_now.at[block_at * block_len : (block_at + 1) * block_len].set(
                block_grad
            )
            return (attn_now, value_now)

        attn_total, value_part = forward_block((attn_total, value_part))
    attn_b = attn_total.astype(jnp.bfloat16)
    delta = jnp.sum(out_heads.astype(jnp.float32) * attn_b.astype(jnp.float32), axis=-1)
    delta = delta.transpose(1, 2, 0)[..., None]
    dnormed = jnp.zeros((text_rows, kv_here, group_size, head_dim), jnp.float32)
    key_part = jnp.zeros((keys_all.shape[0], kv_here, head_dim), jnp.float32)
    for block_at in range(MAX_TILES):
        live_flag = block_at < tiles_here

        def backward_block(carry, block_at=block_at, live_flag=live_flag):
            query_now, key_now = carry
            probs = probs_of(block_at, live_flag)
            key_block = keys_all[block_at * block_len : (block_at + 1) * block_len]
            value_block = values_all[block_at * block_len : (block_at + 1) * block_len]
            dprobs = jnp.einsum(
                "tkgd,jkd->kgtj", out_heads, value_block, preferred_element_type=jnp.float32
            )
            dscores = (probs * (dprobs - delta)).astype(jnp.bfloat16)
            query_now = query_now + jnp.einsum(
                "kgtj,jkd->tkgd", dscores, key_block, preferred_element_type=jnp.float32
            )
            block_grad = (
                jnp.einsum("kgtj,tkgd->jkd", dscores, normed, preferred_element_type=jnp.float32)
                * score_scale
            )
            key_now = key_now.at[block_at * block_len : (block_at + 1) * block_len].set(block_grad)
            return (query_now, key_now)

        dnormed, key_part = backward_block((dnormed, key_part))
    return (dnormed * score_scale, key_part, value_part)


def local(queries, vision, key_weight, value_weight, query_gain, key_gain, out_grad, tile_count):
    head_dim = query_gain.shape[0]
    samples_here, vision_rows, model_width = vision.shape
    text_rows = queries.shape[1]
    kv_here = key_weight.shape[1] // head_dim
    group_size = queries.shape[2] // head_dim // kv_here
    score_scale = head_dim ** (-0.5)
    flat_vision = vision.reshape(samples_here * vision_rows, model_width)
    key_raw = jnp.dot(flat_vision, key_weight, preferred_element_type=jnp.float32)
    key_raw = key_raw.reshape(samples_here, vision_rows, kv_here, head_dim)
    key_normed, key_inverse = norm_apply(key_raw, key_gain)
    own_keys = key_normed.astype(jnp.bfloat16)
    own_values = jnp.dot(flat_vision, value_weight, preferred_element_type=jnp.float32).astype(
        jnp.bfloat16
    )
    own_values = own_values.reshape(samples_here, vision_rows, kv_here, head_dim)
    keys_all, values_all = (
        lax.all_gather(own_keys, "seq", axis=1, tiled=True),
        lax.all_gather(own_values, "seq", axis=1, tiled=True),
    )
    query_raw = queries.astype(jnp.float32).reshape(
        samples_here, text_rows, kv_here, group_size, head_dim
    )
    query_normed, query_inverse = norm_apply(query_raw, query_gain)
    normed = query_normed.astype(jnp.bfloat16)
    out_heads = out_grad.reshape(samples_here, text_rows, kv_here, group_size, head_dim)
    query_list = []
    key_list = []
    value_list = []
    for sample_at in range(samples_here):
        query_part, key_part, value_part = sample_grads(
            normed[sample_at],
            out_heads[sample_at],
            keys_all[sample_at],
            values_all[sample_at],
            tile_count[sample_at],
            score_scale,
        )
        query_list.append(query_part)
        key_list.append(key_part)
        value_list.append(value_part)
    key_sum, value_sum = (
        lax.psum_scatter(
            jnp.stack(key_list).astype(jnp.bfloat16), "seq", scatter_dimension=1, tiled=True
        ).astype(jnp.float32),
        lax.psum_scatter(
            jnp.stack(value_list).astype(jnp.bfloat16), "seq", scatter_dimension=1, tiled=True
        ).astype(jnp.float32),
    )
    key_grad = norm_back(key_raw, key_inverse, key_gain, key_sum).astype(jnp.bfloat16)
    value_grad = value_sum.astype(jnp.bfloat16)
    query_grad = norm_back(query_raw, query_inverse, query_gain, jnp.stack(query_list))
    query_grad = query_grad.astype(jnp.bfloat16).reshape(queries.shape)
    key_flat = key_grad.reshape(samples_here * vision_rows, kv_here * head_dim)
    value_flat = value_grad.reshape(samples_here * vision_rows, kv_here * head_dim)
    heads_key, heads_value = (
        lax.all_gather(key_grad, "mp", axis=2, tiled=True),
        lax.all_gather(value_grad, "mp", axis=2, tiled=True),
    )
    rows_key, rows_value = (
        lax.all_to_all(key_weight, "mp", split_axis=0, concat_axis=1, tiled=True),
        lax.all_to_all(value_weight, "mp", split_axis=0, concat_axis=1, tiled=True),
    )
    every_head = heads_key.shape[2] * head_dim
    vision_part = jnp.einsum(
        "rc,dc->rd",
        heads_key.reshape(samples_here * vision_rows, every_head),
        rows_key,
        preferred_element_type=jnp.float32,
    )
    vision_part = vision_part + jnp.einsum(
        "rc,dc->rd",
        heads_value.reshape(samples_here * vision_rows, every_head),
        rows_value,
        preferred_element_type=jnp.float32,
    )
    vision_grad = vision_part.astype(jnp.bfloat16).reshape(
        samples_here, vision_rows, vision_part.shape[1]
    )
    key_weight_local = jnp.einsum(
        "rd,rc->dc", flat_vision, key_flat, preferred_element_type=jnp.float32
    )
    value_weight_local = jnp.einsum(
        "rd,rc->dc", flat_vision, value_flat, preferred_element_type=jnp.float32
    )
    key_weight_grad, value_weight_grad = (
        lax.psum(key_weight_local.astype(jnp.bfloat16), ("dp", "seq")).astype(jnp.float32),
        lax.psum(value_weight_local.astype(jnp.bfloat16), ("dp", "seq")).astype(jnp.float32),
    )
    return (query_grad, vision_grad, key_weight_grad, value_weight_grad)


def solution(mesh):
    in_specs = (
        P("dp", "seq", "mp"),
        P("dp", "seq", None),
        P(None, "mp"),
        P(None, "mp"),
        P(),
        P(),
        P("dp", "seq", "mp"),
        P("dp"),
    )
    out_specs = (P("dp", "seq", "mp"), P("dp", "seq", "mp"), P(None, "mp"), P(None, "mp"))
    return jax.shard_map(local, mesh=mesh, in_specs=in_specs, out_specs=out_specs, check_vma=False)
```

profile of v0, /device:TPU:0, one launch (start us, length us, event | category | flops | bytes accessed | tf_op | source)
XLA Modules:
  0.0 458.0 jit_solution(17486867492207146060)
XLA Ops:
  7.2 6.4 %copy.174 = bf16[512,4096]{1,0:T(8,128)(2,1)} copy(bf16[512,4096]{0,1:T(8,128)(2,1)} %bitcast.564) | data formatting | bytes 8388608 | tf_op jit(solution)/shard_map/dot_general | solution.py:117
  13.6 3.9 multiply_reduce_fusion.2
  18.4 5.6 %all-to-all-start.1 = ((bf16[2,2048,512]{2,1,0:T(8,128)(2,1)}), bf16[2,2048,512]{2,1,0:T(8,128)(2,1)}, u32[]{:S(2)}, u32[]{:S(2)}) async-start(bf16[2,2048,512]{2,1,0:T(8,128)(2,1)} %bitcast.563), calls=%async_computation.3 | async-start | bytes 8388608 | tf_op jit(solution)/shard_map/all_to_all | solution.py:170
  24.1 3.0 convolution_convert_fusion.2
  33.8 1.6 copy.74
  35.4 2.5 fusion.117
  37.9 2.1 copy.175
  41.0 1.6 multiply_reduce_fusion
  42.6 3.0 copy.77
  45.6 2.2 multiply_convert_fusion
  47.8 16.0 %all-gather.3.cloned.1.call-done = bf16[2,640,4,128]{3,1,2,0:T(8,128)(2,1)} async-done(((bf16[2,80,4,128]{3,1,2,0:T(8,128)(2,1)}), bf16[2,640,4,128]{3,1,2,0:T(8,128)(2,1)}) %all-gather.3.cloned.1.call-update) | async-done | bytes 1310736 | tf_op jit(solution)/shard_map/all_gather | solution.py:126
  71.6 36.1 %all-gather.5.cloned.1.call-done = bf16[2,640,4,128]{3,1,2,0:T(8,128)(2,1)} async-done(((bf16[2,80,4,128]{3,1,2,0:T(8,128)(2,1)}), bf16[2,640,4,128]{3,1,2,0:T(8,128)(2,1)}) %all-gather.5.cloned.1.call-update) | async-done | bytes 1310736 | tf_op jit(solution)/shard_map/all_gather | solution.py:127
  107.6 1.9 fusion.94
  129.8 1.8 convolution_bitcast_fusion.23
  139.9 5.6 %all-to-all-start = ((bf16[2,2048,512]{2,1,0:T(8,128)(2,1)}), bf16[2,2048,512]{2,1,0:T(8,128)(2,1)}, u32[]{:S(2)}, u32[]{:S(2)}) async-start(bf16[2,2048,512]{2,1,0:T(8,128)(2,1)} %bitcast.565), calls=%async_computation.1 | async-start | bytes 8388608 | tf_op jit(solution)/shard_map/all_to_all | solution.py:169
  145.6 47.1 %reduce-scatter.3.cloned.1.call-done = bf16[2,80,4,128]{3,1,2,0:T(8,128)(2,1)} async-done(((bf16[2,640,4,128]{3,1,2,0:T(8,128)(2,1)}), bf16[2,80,4,128]{3,1,2,0:T(8,128)(2,1)}) %reduce-scatter.3.cloned.1.call-update) | async-done | bytes 163856 | tf_op jit(solution)/shard_map/reduce_scatter | solution.py:151
  195.8 64.9 %reduce-scatter.5.cloned.1.call-done = bf16[2,80,4,128]{3,1,2,0:T(8,128)(2,1)} async-done(((bf16[2,640,4,128]{3,1,2,0:T(8,128)(2,1)}), bf16[2,80,4,128]{3,1,2,0:T(8,128)(2,1)}) %reduce-scatter.5.cloned.1.call-update) | async-done | bytes 163856 | tf_op jit(solution)/shard_map/reduce_scatter | solution.py:154
  261.7 3.2 fusion
  264.9 3.2 fusion.1
  268.2 6.6 %copy.111 = bf16[2048,2,512]{0,2,1:T(8,128)(2,1)} copy(bf16[2048,2,512]{2,0,1:T(8,128)(2,1)} %bitcast.180) | data formatting | bytes 8388608 | tf_op jit(solution)/shard_map/all_to_all | solution.py:170
  274.9 6.2 %copy.101 = bf16[2048,2,512]{0,2,1:T(8,128)(2,1)} copy(bf16[2048,2,512]{2,0,1:T(8,128)(2,1)} %bitcast.145) | data formatting | bytes 8388608 | tf_op jit(solution)/shard_map/all_to_all | solution.py:169
  284.1 1.5 convolution_add_fusion.2
  293.3 2.4 fusion.33
  295.8 2.7 copy.88
  298.5 2.4 fusion.7
  303.0 6.0 %all_gather.15 = bf16[2,80,8,128]{3,1,2,0:T(8,128)(2,1)S(1)} all-gather(bf16[2,80,4,128]{3,1,2,0:T(8,128)(2,1)S(1)} %copy-done.31), channel_id=1, replica_groups=mesh['dp'=2,'seq'=8,'mp'=2] {'mp'}, dimensions={2}, use_global_device_ids=true | all-gather | bytes 491520 | tf_op jit(solution)/shard_map/all_gather | solution.py:166
  309.1 6.0 %all_gather.14 = bf16[2,80,8,128]{3,1,2,0:T(8,128)(2,1)S(1)} all-gather(bf16[2,80,4,128]{3,1,2,0:T(8,128)(2,1)S(1)} %copy-done.28), channel_id=1, replica_groups=mesh['dp'=2,'seq'=8,'mp'=2] {'mp'}, dimensions={2}, use_global_device_ids=true | all-gather | bytes 491520 | tf_op jit(solution)/shard_map/all_gather | solution.py:165
  315.2 3.3 fusion.84
  318.9 1.7 fusion.2
  320.6 116.8 %all-reduce.7.cloned.1.call-done = (bf16[4096,512]{0,1:T(8,128)(2,1)}, bf16[4096,512]{0,1:T(8,128)(2,1)}) async-done(((bf16[4096,512]{0,1:T(8,128)(2,1)}, bf16[4096,512]{0,1:T(8,128)(2,1)}), (bf16[4096,512]{0,1:T(8,128)(2,1)}, bf16[4096,512]{0,1:T(8,128)(2,1)})) %all-reduce.7.cloned.1.call-update) | async-done | bytes 8388624 | tf_op jit(solution)/shard_map/psum | solution.py:195
  437.4 7.0 %copy.115 = f32[4096,512]{1,0:T(8,128)} copy(bf16[4096,512]{0,1:T(8,128)(2,1)} %get-tuple-element.208) | data formatting | bytes 12582912
  444.4 7.0 %copy.116 = f32[4096,512]{1,0:T(8,128)} copy(bf16[4096,512]{0,1:T(8,128)(2,1)} %get-tuple-element.209) | data formatting | bytes 12582912
  (201 shorter events, 56.3 us)
Async XLA Ops:
  7.2 6.5 %copy-start = (bf16[2,80,4096]{2,1,0:T(8,128)(2,1)S(1)}, bf16[2,80,4096]{2,1,0:T(8,128)(2,1)}, u32[]{:S(2)}) copy-start(bf16[2,80,4096]{2,1,0:T(8,128)(2,1)} %param.41) | copy-start | bytes 3932164
  7.2 56.7 %all-gather.3.cloned.1.call-start = ((), (), s32[]{:S(2)}) async-start(), calls=%async_computation.4 | async-start | bytes 1474560 | tf_op jit(solution)/shard_map/all_gather | solution.py:126
  13.6 3.9 copy-start.51
  18.4 121.5 %all-to-all-start.1 = ((bf16[2,2048,512]{2,1,0:T(8,128)(2,1)}), bf16[2,2048,512]{2,1,0:T(8,128)(2,1)}, u32[]{:S(2)}, u32[]{:S(2)}) async-start(bf16[2,2048,512]{2,1,0:T(8,128)(2,1)} %bitcast.563), calls=%async_computation.3 | async-start | bytes 8388608 | tf_op jit(solution)/shard_map/all_to_all | solution.py:170
  24.1 83.6 %all-gather.5.cloned.1.call-start = ((), (), s32[]{:S(2)}) async-start(), calls=%async_computation.5 | async-start | bytes 1474560 | tf_op jit(solution)/shard_map/all_gather | solution.py:127
  24.1 3.9 copy-start.54
  27.9 164.8 %reduce-scatter.3.cloned.1.call-start = ((), (), s32[]{:S(2)}) async-start(), calls=%async_computation.6 | async-start | bytes 1474560 | tf_op jit(solution)/shard_map/reduce_scatter | solution.py:151
  35.4 5.6 %copy-start.3 = (bf16[2,128,2048]{1,2,0:T(8,128)(2,1)}, bf16[2,128,2048]{1,2,0:T(8,128)(2,1)S(1)}, u32[]{:S(2)}) copy-start(bf16[2,128,2048]{1,2,0:T(8,128)(2,1)S(1)} %copy.74) | copy-start | bytes 3145732
  42.6 3.0 copy-start.52
  65.1 5.0 %copy-start.7 = (f32[4,4,128,160]{2,3,1,0:T(8,128)}, f32[4,4,128,160]{2,3,1,0:T(8,128)S(1)}, u32[]{:S(2)}) copy-start(f32[4,4,128,160]{2,3,1,0:T(8,128)S(1)} %get-tuple-element.227) | copy-start | bytes 3932164
  66.6 3.6 copy-start.10
  68.1 2.1 copy-start.13
  107.6 2.0 copy-start.14
  107.6 2.2 copy-start.55
  116.0 10.2 %copy-start.16 = (f32[4,4,128,160]{2,3,1,0:T(8,128)}, f32[4,4,128,160]{2,3,1,0:T(8,128)S(1)}, u32[]{:S(2)}) copy-start(f32[4,4,128,160]{2,3,1,0:T(8,128)S(1)} %get-tuple-element.235) | copy-start | bytes 3932164
  116.4 8.9 %copy-start.18 = (f32[4,4,128,160]{2,3,1,0:T(8,128)}, f32[4,4,128,160]{2,3,1,0:T(8,128)S(1)}, u32[]{:S(2)}) copy-start(f32[4,4,128,160]{2,3,1,0:T(8,128)S(1)} %get-tuple-element.237) | copy-start | bytes 3932164
  116.8 7.4 %copy-start.20 = (f32[4,4,128,160]{2,3,1,0:T(8,128)}, f32[4,4,128,160]{2,3,1,0:T(8,128)S(1)}, u32[]{:S(2)}) copy-start(f32[4,4,128,160]{2,3,1,0:T(8,128)S(1)} %get-tuple-element.239) | copy-start | bytes 3932164
  117.1 3.5 copy-start.22
  118.3 8.0 %copy-start.49 = (f32[4,4,128]{2,1,0:T(4,128)}, f32[4,4,128]{2,1,0:T(4,128)S(1)}, u32[]{:S(2)}) copy-start(f32[4,4,128]{2,1,0:T(4,128)S(1)} %multiply_add_fusion.1) | copy-start | bytes 24580
  128.8 131.9 %reduce-scatter.5.cloned.1.call-start = ((), (), s32[]{:S(2)}) async-start(), calls=%async_computation.7 | async-start | bytes 1474560 | tf_op jit(solution)/shard_map/reduce_scatter | solution.py:154
  129.8 1.9 copy-start.15
  129.8 1.9 copy-start.48
  139.9 134.9 %all-to-all-start = ((bf16[2,2048,512]{2,1,0:T(8,128)(2,1)}), bf16[2,2048,512]{2,1,0:T(8,128)(2,1)}, u32[]{:S(2)}, u32[]{:S(2)}) async-start(bf16[2,2048,512]{2,1,0:T(8,128)(2,1)} %bitcast.565), calls=%async_computation.1 | async-start | bytes 8388608 | tf_op jit(solution)/shard_map/all_to_all | solution.py:169
  145.6 291.8 %all-reduce.7.cloned.1.call-start = ((), (), s32[]{:S(2)}) async-start(), calls=%async_computation.8 | async-start | bytes 16777216 | tf_op jit(solution)/shard_map/psum | solution.py:195
  287.1 3.1 copy-start.5
  295.8 2.7 copy-start.1
  295.8 2.7 copy-start.53
  298.5 2.4 copy-start.4
  298.5 2.4 copy-start.25
  298.5 2.5 copy-start.26
  301.7 7.4 %copy-start.28 = (bf16[2,80,4,128]{3,1,2,0:T(8,128)(2,1)S(1)}, bf16[2,80,4,128]{3,1,2,0:T(8,128)(2,1)}, u32[]{:S(2)}) copy-start(bf16[2,80,4,128]{3,1,2,0:T(8,128)(2,1)} %copy-done.27) | copy-start | bytes 491524
  315.2 3.7 copy-start.2
  (31 other events, 38.1 us)
Sparse Core Ops, SparseCore 0:
  18.6 45.2 all-gather.2
  66.6 40.9 all-gather.4
  128.9 63.7 reduce-scatter.2
  196.6 64.0 reduce-scatter.4
  268.3 169.0 all-reduce.6
where the time goes:
time: 460 us; the launch traced here: 458 us
  waiting for transfers between devices  281 us (61%)
  local copies, waits for them, and re-layouts  64.2 us (14%)
  matrix products  54.9 us (12%)
  between operations  19.9 us (4%)
  other arithmetic  14.5 us (3%)
  blocking collectives  12 us (3%)
  starting transfers between devices  11.5 us (2%)
    psum x1, waiting for transfers between devices, local(): lax.psum(key_weight_local.astype(jnp.bfloat16), ('dp', 'seq'))  117 us
    reduce_scatter x1, waiting for transfers between devices, local(): lax.psum_scatter(jnp.stack(value_list).astype(jnp.bfloat16), 'seq', scatt...  64.9 us
    reduce_scatter x1, waiting for transfers between devices, local(): lax.psum_scatter(jnp.stack(key_list).astype(jnp.bfloat16), 'seq', scatter...  47.1 us
    all_gather x1, waiting for transfers between devices, local(): lax.all_gather(own_values, 'seq', axis=1, tiled=True)  36.1 us
    unnamed x118, local copies, waits for them, and re-layouts  32.8 us
    all_gather x1, waiting for transfers between devices, local(): lax.all_gather(own_keys, 'seq', axis=1, tiled=True)  16 us
    dot_general x8, matrix products, backward_block(): jnp.einsum('kgtj,jkd->tkgd', dscores, key_block, preferred_element_type=j...  13 us
  transfers between devices with their start and end apart: 7, of which 5 were waited for; matrix products, arithmetic and copies ran while one was open for 21% of the time, Pallas kernels for 0%

commit v1 on v0

v1 whole, which is shorter than its diff:
```python
import functools

import jax
import jax.numpy as jnp
from jax import lax
from jax.experimental import pallas as pl
from jax.experimental.pallas import tpu as pltpu
from jax.sharding import PartitionSpec as P

MAX_TILES = 4
EPS = 1e-05
NEG = -1e30
MESH = pl.DeviceIdType.MESH
VMEM = pltpu.VMEM
F32 = jnp.float32
BF16 = jnp.bfloat16
CHUNKS = 2


def norm_back(raw, inverse, gain, upstream):
    weighted = upstream * gain
    return inverse * weighted - raw * inverse * inverse * inverse * jnp.mean(
        weighted * raw, axis=-1, keepdims=True
    )


def inverse_of(raw):
    return lax.rsqrt(jnp.mean(raw * raw, axis=-1, keepdims=True) + EPS)


def seq_of(place, n):
    half = place // (n // 2)
    along = place + half * (n - 1 - 2 * place)
    return 2 * along + half


def place_of(index, n):
    side = index % 2
    along = index // 2
    return along + side * (n - 1 - 2 * along)


def ring(n):
    here = lax.axis_index("seq")
    place = place_of(here, n)
    nexts = (seq_of((place + 1) % n, n), seq_of((place + n - 1) % n, n))
    return here, place, nexts


def greet(devices):
    barrier = pltpu.get_barrier_semaphore()
    for device in devices:
        pl.semaphore_signal(barrier, inc=1, device_id=device, device_id_type=MESH)
    pl.semaphore_wait(barrier, len(devices))


def gather_kernel(n, pairs, *refs):
    sources, outs = refs[0:2], refs[2:4]
    send_sem, recv_sem, pair_send, pair_recv = refs[4:8]
    here, place, nexts = ring(n)
    mine = lax.axis_index("dp")
    chunks = sources[0].shape[0]
    others = [(mine + shift) % pairs for shift in range(1, pairs)]
    greet([{"seq": nexts[0]}, {"seq": nexts[1]}] + [{"dp": other} for other in others])
    ring_copies, pair_copies = [], []
    for step in range(n):
        for chunk in range(chunks):
            for way in range(2):
                origin = seq_of((place + n - step) % n if way == 0 else (place + step) % n, n)
                target = outs[way].at[mine if pairs > 1 else 0, chunk, origin]
                if step == 0:
                    block = sources[way].at[chunk]
                else:
                    ring_copies[((step - 1) * chunks + chunk) * 2 + way].wait_recv()
                    block = target
                if step < n - 1:
                    copy = pltpu.make_async_remote_copy(
                        src_ref=block,
                        dst_ref=target,
                        send_sem=send_sem.at[way, step, chunk],
                        recv_sem=recv_sem.at[way, step, chunk],
                        device_id={"seq": nexts[way]},
                        device_id_type=MESH,
                    )
                    copy.start()
                    ring_copies.append(copy)
                for at, other in enumerate(others):
                    copy = pltpu.make_async_remote_copy(
                        src_ref=block,
                        dst_ref=target,
                        send_sem=pair_send.at[way, step, chunk, at],
                        recv_sem=pair_recv.at[way, step, chunk, at],
                        device_id={"dp": other},
                        device_id_type=MESH,
                    )
                    copy.start()
                    pair_copies.append(copy)
        if step == 0:
            for way in range(2):
                for chunk in range(chunks):
                    outs[way][mine if pairs > 1 else 0, chunk, here] = sources[way][chunk]
    for copy in ring_copies:
        copy.wait_send()
    for copy in pair_copies:
        copy.wait_send()
        copy.wait_recv()


def ring_gather(first, second, n, pairs, number):
    chunks, rows, columns = first.shape
    out = jax.ShapeDtypeStruct((pairs, chunks, n, rows, columns), first.dtype)
    sent = 2 * chunks * (n - 1) * rows * columns * 2
    return pl.pallas_call(
        functools.partial(gather_kernel, n, pairs),
        out_shape=(out, out),
        in_specs=[pl.BlockSpec(memory_space=VMEM)] * 2,
        out_specs=(pl.BlockSpec(memory_space=VMEM),) * 2,
        scratch_shapes=[
            pltpu.SemaphoreType.DMA((2, n, chunks)),
            pltpu.SemaphoreType.DMA((2, n, chunks)),
            pltpu.SemaphoreType.DMA((2, n, chunks, max(pairs - 1, 1))),
            pltpu.SemaphoreType.DMA((2, n, chunks, max(pairs - 1, 1))),
        ],
        compiler_params=pltpu.CompilerParams(collective_id=number, has_side_effects=True),
        cost_estimate=pl.CostEstimate(flops=100_000_000_000 // 4, bytes_accessed=sent, transcendentals=0),
        name=f"ring_gather_{number}",
    )(first, second)


def scatter_kernel(n, head_dim, key_ref, value_ref, raw_ref, gain_ref, key_out, value_out, *scratch):
    held, send_sem, recv_sem = scratch
    parts = (key_ref, value_ref)
    here, place, nexts = ring(n)
    chunks = key_ref.shape[0]
    greet([{"seq": nexts[0]}, {"seq": nexts[1]}])

    def copy_of(way, step, chunk, block):
        return pltpu.make_async_remote_copy(
            src_ref=block,
            dst_ref=held.at[way, step, chunk],
            send_sem=send_sem.at[way, step, chunk],
            recv_sem=recv_sem.at[way, step, chunk],
            device_id={"seq": nexts[way]},
            device_id_type=MESH,
        )

    def dest_of(way, step):
        if way == 0:
            return seq_of((place + 2 * n - 1 - step) % n, n)
        return seq_of((place + 1 + step) % n, n)

    copies = {}
    for chunk in range(chunks):
        for way in range(2):
            copy = copy_of(way, 0, chunk, parts[way].at[chunk, dest_of(way, 0)])
            copy.start()
            copies[way, 0, chunk] = copy
    for step in range(1, n):
        for chunk in range(chunks):
            for way in range(2):
                copies[way, step - 1, chunk].wait_recv()
                own = parts[way][chunk, dest_of(way, step)].astype(F32)
                total = held[way, step - 1, chunk].astype(F32) + own
                if step < n - 1:
                    held[way, step - 1, chunk] = total.astype(BF16)
                elif way == 1:
                    value_out[chunk] = total.astype(BF16)
                else:
                    gain = gain_ref[...]
                    for at in range(total.shape[1] // head_dim):
                        cut = slice(at * head_dim, (at + 1) * head_dim)
                        raw = raw_ref[chunk, :, cut]
                        grad = norm_back(raw, inverse_of(raw), gain, total[:, cut])
                        key_out[chunk, :, cut] = grad.astype(BF16)
            if step < n - 1:
                for way in range(2):
                    copy = copy_of(way, step, chunk, held.at[way, step - 1, chunk])
                    copy.start()
                    copies[way, step, chunk] = copy
    for copy in copies.values():
        copy.wait_send()


def ring_scatter(key_part, value_part, key_raw, gain, number):
    chunks, n, rows, columns = key_part.shape
    out = jax.ShapeDtypeStruct((chunks, rows, columns), BF16)
    sent = 2 * chunks * (n - 1) * rows * columns * 2
    return pl.pallas_call(
        functools.partial(scatter_kernel, n, gain.shape[1]),
        out_shape=(out, out),
        in_specs=[pl.BlockSpec(memory_space=VMEM)] * 4,
        out_specs=(pl.BlockSpec(memory_space=VMEM),) * 2,
        scratch_shapes=[
            pltpu.VMEM((2, n - 1, chunks, rows, columns), BF16),
            pltpu.SemaphoreType.DMA((2, n - 1, chunks)),
            pltpu.SemaphoreType.DMA((2, n - 1, chunks)),
        ],
        compiler_params=pltpu.CompilerParams(collective_id=number, has_side_effects=True),
        cost_estimate=pl.CostEstimate(flops=100_000_000_000 // 4, bytes_accessed=sent, transcendentals=0),
        name="ring_scatter",
    )(key_part, value_part, key_raw, gain)


def norm_kernel(head_dim, raw_ref, gain_ref, out_ref):
    gain = gain_ref[...]
    for at in range(raw_ref.shape[-1] // head_dim):
        cut = slice(at * head_dim, (at + 1) * head_dim)
        raw = raw_ref[:, :, cut]
        out_ref[:, :, cut] = (raw * inverse_of(raw) * gain).astype(BF16)


def attention_kernel(group, tile_tokens, tiles_ref, query_ref, grad_ref, key_ref, value_ref, gain_ref,
                     query_out, key_out, value_out):
    text_rows = query_ref.shape[1]
    head_dim = key_ref.shape[2]
    scale = head_dim ** (-0.5)
    live = tiles_ref[pl.program_id(0)] * tile_tokens

    def stacked(ref):
        return jnp.concatenate(
            [ref[0, :, at * head_dim : (at + 1) * head_dim] for at in range(group)], axis=0
        )

    def mul(left, right, dims):
        return lax.dot_general(left, right, (dims, ((), ())), preferred_element_type=F32)

    raw = stacked(query_ref).astype(F32)
    outs = stacked(grad_ref)
    gain = gain_ref[...]
    inverse = inverse_of(raw)
    normed = (raw * inverse * gain).astype(BF16)
    keys = key_ref[0]
    values = value_ref[0]
    scores = mul(normed, keys, ((1,), (1,))) * scale
    token = lax.broadcasted_iota(jnp.int32, scores.shape, 1)
    scores = jnp.where(token < live, scores, NEG)
    expo = jnp.exp(scores - jnp.max(scores, axis=-1, keepdims=True))
    probs = expo * (1.0 / jnp.sum(expo, axis=-1, keepdims=True))
    probs_b = probs.astype(BF16)
    attn = mul(probs_b, values, ((1,), (0,))).astype(BF16)
    delta = jnp.sum(outs.astype(F32) * attn.astype(F32), axis=-1, keepdims=True)
    dprobs = mul(outs, values, ((1,), (1,)))
    dscores = (probs * (dprobs - delta)).astype(BF16)
    value_out[0] = mul(probs_b, outs, ((0,), (0,))).astype(BF16)
    key_out[0] = (mul(dscores, normed, ((0,), (0,))) * scale).astype(BF16)
    dnormed = mul(dscores, keys, ((1,), (0,))) * scale
    back = norm_back(raw, inverse, gain, dnormed).astype(BF16)
    for at in range(group):
        query_out[0, :, at * head_dim : (at + 1) * head_dim] = back[at * text_rows : (at + 1) * text_rows]


def attention(tiles, queries, out_grad, keys, values, gain):
    samples, text_rows, query_width = queries.shape
    tokens, key_width = keys.shape[1:]
    head_dim = gain.shape[1]
    heads = key_width // head_dim
    group = query_width // key_width
    wide = pl.BlockSpec((1, text_rows, group * head_dim), lambda s, h: (s, 0, h))
    tall = pl.BlockSpec((1, tokens, head_dim), lambda s, h: (s, 0, h))
    flops = samples * query_width * text_rows * tokens * 10
    part = jax.ShapeDtypeStruct((samples, tokens, key_width), BF16)
    return pl.pallas_call(
        functools.partial(attention_kernel, group, tokens // MAX_TILES),
        grid=(samples, heads),
        out_shape=(jax.ShapeDtypeStruct(queries.shape, BF16), part, part),
        in_specs=[
            pl.BlockSpec(memory_space=pltpu.SMEM),
            wide,
            wide,
            tall,
            tall,
            pl.BlockSpec((1, head_dim), lambda s, h: (0, 0)),
        ],
        out_specs=(wide, tall, tall),
        compiler_params=pltpu.CompilerParams(vmem_limit_bytes=48 * 1024 * 1024),
        cost_estimate=pl.CostEstimate(flops=flops, bytes_accessed=8_000_000, transcendentals=0),
        name="attention",
    )(tiles, queries, out_grad, keys, values, gain)


def local(sizes, queries, vision, key_weight, value_weight, query_gain, key_gain, out_grad, tile_count):
    pairs, n, heads_cut = sizes
    head_dim = query_gain.shape[0]
    samples, rows, model_width = vision.shape
    columns = key_weight.shape[1]
    flat_vision = vision.reshape(samples * rows, model_width)

    shard = model_width // (pairs * CHUNKS * n)
    cut = flat_vision.reshape(samples * rows, pairs, CHUNKS, n, shard)
    cut = cut.transpose(1, 3, 0, 2, 4).reshape(pairs * n, samples * rows, CHUNKS * shard)
    column_vision = lax.all_to_all(cut, ("dp", "seq"), split_axis=0, concat_axis=0, tiled=True)
    column_vision = column_vision.reshape(pairs, n, samples, rows, CHUNKS * shard)
    column_vision = column_vision.transpose(0, 2, 1, 3, 4).reshape(-1, CHUNKS * shard)

    key_raw = jnp.dot(flat_vision, key_weight, preferred_element_type=F32)
    key_raw = key_raw.reshape(samples, rows, columns)
    own_values = jnp.dot(flat_vision, value_weight, preferred_element_type=F32).astype(BF16)
    own_values = own_values.reshape(samples, rows, columns)
    own_keys = pl.pallas_call(
        functools.partial(norm_kernel, head_dim),
        out_shape=jax.ShapeDtypeStruct(key_raw.shape, BF16),
        name="key_norm",
    )(key_raw, key_gain[None])
    keys_all, values_all = ring_gather(own_keys, own_values, n, 1, 1)
    keys_all = keys_all.reshape(samples, n * rows, columns)
    values_all = values_all.reshape(samples, n * rows, columns)
    query_grad, key_part, value_part = attention(
        tile_count, queries, out_grad, keys_all, values_all, query_gain[None]
    )
    key_grad, value_grad = ring_scatter(
        key_part.reshape(samples, n, rows, columns),
        value_part.reshape(samples, n, rows, columns),
        key_raw,
        key_gain[None],
        2,
    )

    share = model_width // heads_cut
    vision_part = jnp.einsum(
        "rc,dc->rd", key_grad.reshape(samples * rows, columns), key_weight, preferred_element_type=F32
    ) + jnp.einsum(
        "rc,dc->rd", value_grad.reshape(samples * rows, columns), value_weight, preferred_element_type=F32
    )
    me = lax.axis_index("mp")
    total = lax.dynamic_slice_in_dim(vision_part, me * share, share, axis=1)
    for shift in range(1, heads_cut):
        leaving = lax.dynamic_slice_in_dim(
            vision_part, lax.rem(me + shift, heads_cut) * share, share, axis=1
        ).astype(BF16)
        arrived = lax.ppermute(leaving, "mp", [(at, (at + shift) % heads_cut) for at in range(heads_cut)])
        total = total + arrived.astype(F32)
    vision_grad = total.astype(BF16).reshape(samples, rows, share)

    every_key, every_value = ring_gather(key_grad, value_grad, n, pairs, 3)
    outs = []
    for every in (every_key, every_value):
        grad = jnp.einsum(
            "td,tc->dc", column_vision, every.reshape(-1, columns), preferred_element_type=F32
        )
        outs.append(grad.astype(BF16).reshape(CHUNKS, shard, columns))
    key_rows, value_rows = ring_gather(outs[0], outs[1], n, pairs, 4)
    return (
        query_grad,
        vision_grad,
        key_rows.reshape(model_width, columns).astype(F32),
        value_rows.reshape(model_width, columns).astype(F32),
    )


def solution(mesh):
    sizes = (mesh.shape["dp"], mesh.shape["seq"], mesh.shape["mp"])
    in_specs = (
        P("dp", "seq", "mp"),
        P("dp", "seq", None),
        P(None, "mp"),
        P(None, "mp"),
        P(),
        P(),
        P("dp", "seq", "mp"),
        P("dp"),
    )
    out_specs = (P("dp", "seq", "mp"), P("dp", "seq", "mp"), P(None, "mp"), P(None, "mp"))
    return jax.shard_map(
        functools.partial(local, sizes), mesh=mesh, in_specs=in_specs, out_specs=out_specs, check_vma=False
    )
```

time: 460 us -> 245 us (0.53)
  waiting for transfers between devices: 281 us -> 0.01 us
  Pallas kernels: 0 us -> 189 us
  local copies, waits for them, and re-layouts: 64.2 us -> 9.6 us
  matrix products: 54.9 us -> 21.8 us
  between operations: 19.9 us -> 0.83 us
  blocking collectives: 12 us -> 0 us
    pallas_call x0 -> x6, Pallas kernels: none -> 189 us  [the longest x3 137 us: ring_gather(): pl.pallas_call(functools.partial(gather_kernel, n, pairs), out_shape=(out...]
    psum x1 -> x0, waiting for transfers between devices: 117 us -> none  [local(): lax.psum(key_weight_local.astype(jnp.bfloat16), ('dp', 'seq'))]
    reduce_scatter x2 -> x0, waiting for transfers between devices: 112 us -> none  [the longest x1 64.9 us: local(): lax.psum_scatter(jnp.stack(value_list).astype(jnp.bfloat16), 'seq', scatt...]
    all_gather x2 -> x0, waiting for transfers between devices: 52.1 us -> none  [the longest x1 36.1 us: local(): lax.all_gather(own_values, 'seq', axis=1, tiled=True)]
    dot_general x54 -> x6, matrix products: 54.9 us -> 21.8 us  [the longest x2 6.77 us: local(): jnp.einsum('td,tc->dc', column_vision, every.reshape(-1, columns), prefer...]
    unnamed x118 -> x25, local copies, waits for them, and re-layouts: 32.8 us -> 6.54 us
    all_to_all x2 -> x0, local copies, waits for them, and re-layouts: 12.9 us -> none  [the longest x1 6.65 us: local(): lax.all_to_all(value_weight, 'mp', split_axis=0, concat_axis=1, tiled=True)]
    all_gather x2 -> x0, blocking collectives: 12 us -> none  [the longest x1 5.99 us: local(): lax.all_gather(key_grad, 'mp', axis=2, tiled=True)]
  transfers between devices with their start and end apart: 7 -> 2, of which waited for: 5 -> 0; matrix products, arithmetic and copies ran while one was open for 21% -> 7% of each run, Pallas kernels for 0% -> 57%
where the time goes in v1:
time: 245 us
  Pallas kernels  189 us (77%)
  matrix products  21.8 us (9%)
  other arithmetic  14.1 us (6%)
  local copies, waits for them, and re-layouts  9.6 us (4%)
  starting transfers between devices  9.01 us (4%)
    pallas_call x3, Pallas kernels, ring_gather(): pl.pallas_call(functools.partial(gather_kernel, n, pairs), out_shape=(out...  137 us
    pallas_call x1, Pallas kernels, ring_scatter(): pl.pallas_call(functools.partial(scatter_kernel, n, gain.shape[1]), out_s...  32.7 us
    pallas_call x1, Pallas kernels, attention(): pl.pallas_call(functools.partial(attention_kernel, group, tokens // MAX_T...  18.1 us
    convert_element_type x1, other arithmetic, local(): value_rows.reshape(model_width, columns).astype(F32)  12 us
    all_to_all x1, starting transfers between devices, local(): lax.all_to_all(cut, ('dp', 'seq'), split_axis=0, concat_axis=0, tiled=True)  7.43 us
    dot_general x2, matrix products, local(): jnp.einsum('td,tc->dc', column_vision, every.reshape(-1, columns), prefer...  6.77 us
    unnamed x25, local copies, waits for them, and re-layouts  6.54 us
  transfers between devices with their start and end apart: 2, of which 0 were waited for; matrix products, arithmetic and copies ran while one was open for 7% of the time, Pallas kernels for 57%

profile of v1, /device:TPU:0, one launch (start us, length us, event | category | flops | bytes accessed | tf_op | source)
XLA Modules:
  0.0 244.8 jit_solution(17075079716918171004)
XLA Ops:
  0.6 1.6 copy.16
  2.2 1.3 copy.26
  3.5 0.0 copy-start.7
  3.5 1.7 reshape.68
  5.2 7.4 %all-to-all-start = ((bf16[16,160,256]{2,1,0:T(8,128)(2,1)}), bf16[16,160,256]{2,1,0:T(8,128)(2,1)}, u32[]{:S(2)}, u32[]{:S(2)}) async-start(bf16[16,160,256]{2,1,0:T(8,128)(2,1)} %reshape.68), calls=%async_computation | async-start | bytes 2621440 | tf_op jit(solution)/shard_map/all_to_all | solution.py:291
  12.7 3.8 %fusion.raw_ref = f32[2,80,512]{2,1,0:T(8,128)} fusion(bf16[2,80,4096]{2,1,0:T(8,128)(2,1)S(1)} %copy-done.7, bf16[4096,512]{1,0:T(8,128)(2,1)} %param.10), kind=kOutput, calls=%fused_computation.3 | convolution fusion | flops 671088640 | bytes 5832704 | tf_op jit(solution)/shard_map/dot_general | solution.py:295
  16.4 1.8 key_norm.1.refs_0_
  18.3 3.7 %convolution_convert_fusion = bf16[160,512]{1,0:T(8,128)(2,1)} fusion(bf16[160,4096]{1,0:T(8,128)(2,1)S(1)} %bitcast.73, bf16[4096,512]{1,0:T(8,128)(2,1)} %param.11), kind=kOutput, calls=%fused_computation.16 | convolution fusion | flops 671170560 | bytes 5668864 | tf_op jit(solution)/shard_map/dot_general | solution.py:297
  22.0 52.7 %ring_gather_1.1 = (bf16[1,2,8,80,512]{4,3,2,1,0:T(8,128)(2,1)}, bf16[1,2,8,80,512]{4,3,2,1,0:T(8,128)(2,1)}) custom-call(bf16[2,80,512]{2,1,0:T(8,128)(2,1)} %key_norm.1.refs_0_, bf16[2,80,512]{2,1,0:T(8,128)(2,1)} %bitcast.78), custom_call_target="tpu_custom_call" | custom-call | flops 24999999488 | bytes 2293760 | tf_op jit(solution)/shard_map/ring_gather_1/pallas_call | solution.py:113
  74.7 0.0 copy-done
  74.7 0.0 copy-done.1
  74.7 0.0 copy-done.2
  74.8 1.3 copy-done.6
  76.1 18.1 %attention.1 = (bf16[2,128,2048]{2,1,0:T(8,128)(2,1)}, bf16[2,640,512]{2,1,0:T(8,128)(2,1)S(1)}, bf16[2,640,512]{2,1,0:T(8,128)(2,1)S(1)}) custom-call(s32[2]{0:T(128)S(1)} %copy-done.2, bf16[2,128,2048]{2,1,0:T(8,128)(2,1)S(1)} %copy-done, bf16[2,128,2048]{2,1,0:T(8,128)(2,1)S(1)} %copy-done.1, bf16[2,640,512]{2,1,0:T(8,128)(2,1)S(1)} %bitcast.71, ...), custom_call_target="tpu_custom_call" | custom-call | flops 3355443200 | bytes 8000000 | tf_op jit(solution)/shard_map/attention/pallas_call | solution.py:262
  94.2 1.1 copy-done.4
  95.3 1.1 copy-done.5
  96.3 32.7 %ring_scatter.1 = (bf16[2,80,512]{2,1,0:T(8,128)(2,1)}, bf16[2,80,512]{2,1,0:T(8,128)(2,1)}) custom-call(bf16[2,8,80,512]{3,2,1,0:T(8,128)(2,1)} %bitcast.69, bf16[2,8,80,512]{3,2,1,0:T(8,128)(2,1)} %bitcast.70, f32[2,80,512]{2,1,0:T(8,128)} %fusion.raw_ref, f32[1,128]{1,0:T(1,128)} %bitcast.81), custom_call_target="tpu_custom_call" | custom-call | flops 24999999488 | bytes 2293760 | tf_op jit(solution)/shard_map/ring_scatter/pallas_call | solution.py:188
  129.0 3.8 %fusion.20 = f32[160,4096]{1,0:T(8,128)S(1)} fusion(bf16[160,512]{1,0:T(8,128)(2,1)} %bitcast.77, bf16[4096,512]{1,0:T(8,128)(2,1)} %param.10), kind=kOutput, calls=%fused_computation.19 | convolution fusion | flops 671088640 | bytes 6979584 | tf_op jit(solution)/shard_map/rc,dc->rd/dot_general | solution.py:319
  132.8 3.7 %convolution_add_fusion = f32[160,4096]{1,0:T(8,128)S(1)} fusion(f32[160,4096]{1,0:T(8,128)S(1)} %fusion.20, bf16[160,512]{1,0:T(8,128)(2,1)S(1)} %bitcast.79, bf16[4096,512]{1,0:T(8,128)(2,1)} %param.11), kind=kOutput, calls=%fused_computation | convolution fusion | flops 671744000 | bytes 9601024 | tf_op jit(solution)/shard_map/rc,dc->rd/dot_general | solution.py:321
  136.5 0.0 copy-start.8
  136.6 1.5 copy-done.8
  138.0 0.1 dynamic-slice_convert_fusion
  138.1 0.0 copy-start.9
  138.1 1.6 collective-permute-start
  139.7 35.2 %ring_gather_3.1 = (bf16[2,2,8,80,512]{4,3,2,1,0:T(8,128)(2,1)}, bf16[2,2,8,80,512]{4,3,2,1,0:T(8,128)(2,1)}) custom-call(bf16[2,80,512]{2,1,0:T(8,128)(2,1)} %get-tuple-element.20.refs_0_, bf16[2,80,512]{2,1,0:T(8,128)(2,1)} %get-tuple-element.21.refs_1_), custom_call_target="tpu_custom_call" | custom-call | flops 24999999488 | bytes 2293760 | tf_op jit(solution)/shard_map/ring_gather_3/pallas_call | solution.py:113
  174.9 0.0 collective-permute-done
  175.0 2.1 add_convert_fusion
  177.0 0.0 all-to-all-done
  177.0 3.9 %fusion.15 = bf16[512,256]{0,1:T(8,128)(2,1)} fusion(bf16[2,2,8,80,512]{4,3,2,1,0:T(8,128)(2,1)} %get-tuple-element.22, bf16[2,8,2,80,256]{4,3,2,1,0:T(8,128)(2,1)} %bitcast.13), kind=kOutput, calls=%fused_computation.15 | convolution fusion | flops 671219712 | bytes 4194304 | tf_op jit(solution)/shard_map/td,tc->dc/dot_general | solution.py:337
  180.9 2.9 %fusion.12 = bf16[512,256]{0,1:T(8,128)(2,1)} fusion(bf16[2,2,8,80,512]{4,3,2,1,0:T(8,128)(2,1)S(1)} %copy-done.11, bf16[2,8,2,80,256]{4,3,2,1,0:T(8,128)(2,1)} %bitcast.13), kind=kOutput, calls=%fused_computation.14 | convolution fusion | flops 671219712 | bytes 4194304 | tf_op jit(solution)/shard_map/td,tc->dc/dot_general | solution.py:337
  183.8 48.9 %ring_gather_4.1 = (bf16[2,2,8,128,512]{4,3,2,1,0:T(8,128)(2,1)}, bf16[2,2,8,128,512]{4,3,2,1,0:T(8,128)(2,1)}) custom-call(bf16[2,128,512]{2,1,0:T(8,128)(2,1)} %bitcast.83, bf16[2,128,512]{2,1,0:T(8,128)(2,1)} %bitcast.84), custom_call_target="tpu_custom_call" | custom-call | flops 24999999488 | bytes 3670016 | tf_op jit(solution)/shard_map/ring_gather_4/pallas_call | solution.py:113
  232.7 12.0 %bitcast_convert_fusion = (f32[4096,512]{1,0:T(8,128)}, f32[4096,512]{1,0:T(8,128)}) fusion(bf16[2,2,8,128,512]{4,3,2,1,0:T(8,128)(2,1)} %get-tuple-element.25, bf16[2,2,8,128,512]{4,3,2,1,0:T(8,128)(2,1)} %get-tuple-element.24), kind=kLoop, calls=%fused_computation.1 | loop fusion | flops 4194304 | bytes 25165824 | tf_op jit(solution)/shard_map/convert_element_type | solution.py:346
  (14 shorter events, 0.0 us)
Async XLA Ops:
  3.5 9.2 %copy-start.7 = (bf16[2,80,4096]{2,1,0:T(8,128)(2,1)S(1)}, bf16[2,80,4096]{2,1,0:T(8,128)(2,1)}, u32[]{:S(2)}) copy-start(bf16[2,80,4096]{2,1,0:T(8,128)(2,1)} %param.9) | copy-start | bytes 3932164
  5.2 171.8 %all-to-all-start = ((bf16[16,160,256]{2,1,0:T(8,128)(2,1)}), bf16[16,160,256]{2,1,0:T(8,128)(2,1)}, u32[]{:S(2)}, u32[]{:S(2)}) async-start(bf16[16,160,256]{2,1,0:T(8,128)(2,1)} %reshape.68), calls=%async_computation | async-start | bytes 2621440 | tf_op jit(solution)/shard_map/all_to_all | solution.py:291
  22.0 52.8 %copy-start = (bf16[2,128,2048]{2,1,0:T(8,128)(2,1)S(1)}, bf16[2,128,2048]{2,1,0:T(8,128)(2,1)}, u32[]{:S(2)}) copy-start(bf16[2,128,2048]{2,1,0:T(8,128)(2,1)} %query_ref.1) | copy-start | bytes 3145732
  22.0 52.8 %copy-start.1 = (bf16[2,128,2048]{2,1,0:T(8,128)(2,1)S(1)}, bf16[2,128,2048]{2,1,0:T(8,128)(2,1)}, u32[]{:S(2)}) copy-start(bf16[2,128,2048]{2,1,0:T(8,128)(2,1)} %grad_ref.1) | copy-start | bytes 3145732
  22.0 52.8 %copy-start.2 = (s32[2]{0:T(128)S(1)}, s32[2]{0:T(128)}, u32[]{:S(2)}) copy-start(s32[2]{0:T(128)} %tiles_ref.1) | copy-start | bytes 28
  22.0 52.8 %copy-start.3 = (f32[128]{0:T(128)S(1)}, f32[128]{0:T(128)}, u32[]{:S(2)}) copy-start(f32[128]{0:T(128)} %param.12) | copy-start | bytes 1540
  74.8 1.3 copy-start.6
  94.2 1.1 copy-start.4
  95.3 1.1 copy-start.5
  129.0 3.8 %copy-start.10 = (bf16[2,80,512]{2,1,0:T(8,128)(2,1)S(1)}, bf16[2,80,512]{2,1,0:T(8,128)(2,1)}, u32[]{:S(2)}) copy-start(bf16[2,80,512]{2,1,0:T(8,128)(2,1)} %get-tuple-element.21.refs_1_) | copy-start | bytes 491524
  136.5 1.5 copy-start.8
  138.1 36.8 %copy-start.9 = (f32[160,4096]{1,0:T(8,128)S(1)}, f32[160,4096]{1,0:T(8,128)}, u32[]{:S(2)}) copy-start(f32[160,4096]{1,0:T(8,128)} %copy-done.8) | copy-start | bytes 7864324
  138.1 36.8 %collective-permute-start = (bf16[160,2048]{1,0:T(8,128)(2,1)S(1)}, bf16[160,2048]{1,0:T(8,128)(2,1)}, u32[]{:S(2)}, u32[]{:S(2)}) collective-permute-start(bf16[160,2048]{1,0:T(8,128)(2,1)S(1)} %dynamic-slice_convert_fusion), channel_id=1, source_target_pairs={{0,1},{1,0},{2,3},{3,2},{4,5},{5,4},{6,7},{7,6},{8,9},{9,8},{10,11... | collective-permute-start | bytes 1966088 | tf_op jit(solution)/shard_map/ppermute | solution.py:330
  177.0 3.9 %copy-start.11 = (bf16[2,2,8,80,512]{4,3,2,1,0:T(8,128)(2,1)S(1)}, bf16[2,2,8,80,512]{4,3,2,1,0:T(8,128)(2,1)}, u32[]{:S(2)}) copy-start(bf16[2,2,8,80,512]{4,3,2,1,0:T(8,128)(2,1)} %get-tuple-element.23) | copy-start | bytes 7864324

commit v2 on v1

--- a/solution.py
+++ b/solution.py
@@ -14,7 +14,10 @@
 VMEM = pltpu.VMEM
 F32 = jnp.float32
 BF16 = jnp.bfloat16
-CHUNKS = 2
+
+
+def chunks_of(width, pairs, n):
+    return 2 if width % (2 * pairs * n * 128) == 0 else 1
 
 
 def norm_back(raw, inverse, gain, upstream):
@@ -54,56 +57,101 @@
     pl.semaphore_wait(barrier, len(devices))
 
 
-def gather_kernel(n, pairs, *refs):
-    sources, outs = refs[0:2], refs[2:4]
-    send_sem, recv_sem, pair_send, pair_recv = refs[4:8]
+def run_ring(n, pairs, sources, outs, sems, prepare=None, jobs=(), kept=True):
+    send_sem, recv_sem, pair_send, pair_recv = sems
     here, place, nexts = ring(n)
-    mine = lax.axis_index("dp")
+    lane = lax.axis_index("dp") if pairs > 1 else 0
     chunks = sources[0].shape[0]
-    others = [(mine + shift) % pairs for shift in range(1, pairs)]
-    greet([{"seq": nexts[0]}, {"seq": nexts[1]}] + [{"dp": other} for other in others])
-    ring_copies, pair_copies = [], []
-    for step in range(n):
+    others = [(lane + shift) % pairs for shift in range(1, pairs)]
+    ring_copies, pair_copies = {}, []
+    jobs = list(jobs)
+
+    def pass_on(way, step, chunk):
+        origin = seq_of((place + n - step) % n if way == 0 else (place + step) % n, n)
+        target = outs[way].at[lane, chunk, origin] if kept else outs[way].at[chunk, origin]
+        block = sources[way].at[chunk] if step == 0 else target
+        if step > 0:
+            ring_copies[way, step - 1, chunk].wait_recv()
+        if step < n - 1:
+            copy = pltpu.make_async_remote_copy(
+                src_ref=block,
+                dst_ref=target,
+                send_sem=send_sem.at[way, step, chunk],
+                recv_sem=recv_sem.at[way, step, chunk],
+                device_id={"seq": nexts[way]},
+                device_id_type=MESH,
+            )
+            copy.start()
+            ring_copies[way, step, chunk] = copy
+        for at, other in enumerate(others):
+            copy = pltpu.make_async_remote_copy(
+                src_ref=block,
+                dst_ref=target,
+                send_sem=pair_send.at[way, step, chunk, at],
+                recv_sem=pair_recv.at[way, step, chunk, at],
+                device_id={"dp": other},
+                device_id_type=MESH,
+            )
+            copy.start()
+            pair_copies.append(copy)
+
+    for way in range(2):
+        if prepare is not None:
+            prepare(way)
         for chunk in range(chunks):
+            pass_on(way, 0, chunk)
+    for way in range(2):
+        for chunk in range(chunks):
+            if kept:
+                outs[way][lane, chunk, here] = sources[way][chunk]
+            else:
+                outs[way][chunk, here] = sources[way][chunk]
+    for step in range(1, n):
+        for chunk in range(chunks):
+            if jobs:
+                jobs.pop(0)()
             for way in range(2):
-                origin = seq_of((place + n - step) % n if way == 0 else (place + step) % n, n)
-                target = outs[way].at[mine if pairs > 1 else 0, chunk, origin]
-                if step == 0:
-                    block = sources[way].at[chunk]
-                else:
-                    ring_copies[((step - 1) * chunks + chunk) * 2 + way].wait_recv()
-                    block = target
-                if step < n - 1:
-                    copy = pltpu.make_async_remote_copy(
-                        src_ref=block,
-                        dst_ref=target,
-                        send_sem=send_sem.at[way, step, chunk],
-                        recv_sem=recv_sem.at[way, step, chunk],
-                        device_id={"seq": nexts[way]},
-                        device_id_type=MESH,
-                    )
-                    copy.start()
-                    ring_copies.append(copy)
-                for at, other in enumerate(others):
-                    copy = pltpu.make_async_remote_copy(
-                        src_ref=block,
-                        dst_ref=target,
-                        send_sem=pair_send.at[way, step, chunk, at],
-                        recv_sem=pair_recv.at[way, step, chunk, at],
-                        device_id={"dp": other},
-                        device_id_type=MESH,
-                    )
-                    copy.start()
-                    pair_copies.append(copy)
-        if step == 0:
-            for way in range(2):
-                for chunk in range(chunks):
-                    outs[way][mine if pairs > 1 else 0, chunk, here] = sources[way][chunk]
-    for copy in ring_copies:
+                pass_on(way, step, chunk)
+    for job in jobs:
+        job()
+    for copy in ring_copies.values():
         copy.wait_send()
     for copy in pair_copies:
         copy.wait_send()
         copy.wait_recv()
+
+
+def ring_sems(n, pairs, chunks):
+    return [
+        pltpu.SemaphoreType.DMA((2, n, chunks)),
+        pltpu.SemaphoreType.DMA((2, n, chunks)),
+        pltpu.SemaphoreType.DMA((2, n, chunks, max(pairs - 1, 1))),
+        pltpu.SemaphoreType.DMA((2, n, chunks, max(pairs - 1, 1))),
+    ]
+
+
+def greet_ring(n, pairs, mates=()):
+    nexts = ring(n)[2]
+    lane = lax.axis_index("dp")
+    others = [{"dp": (lane + shift) % pairs} for shift in range(1, pairs)]
+    greet([{"seq": nexts[0]}, {"seq": nexts[1]}] + others + list(mates))
+
+
+def size_of(*arrays):
+    return sum(array.size * array.dtype.itemsize for array in arrays)
+
+
+def limit_of(*arrays):
+    return size_of(*arrays) + 4 * 1024 * 1024
+
+
+def cost_of(sent):
+    return pl.CostEstimate(flops=25_000_000_000, bytes_accessed=sent, transcendentals=0)
+
+
+def gather_kernel(n, pairs, first_ref, second_ref, first_out, second_out, *sems):
+    greet_ring(n, pairs)
+    run_ring(n, pairs, (first_ref, second_ref), (first_out, second_out), sems)
 
 
 def ring_gather(first, second, n, pairs, number):
@@ -115,16 +163,284 @@
         out_shape=(out, out),
         in_specs=[pl.BlockSpec(memory_space=VMEM)] * 2,
         out_specs=(pl.BlockSpec(memory_space=VMEM),) * 2,
-        scratch_shapes=[
-            pltpu.SemaphoreType.DMA((2, n, chunks)),
-            pltpu.SemaphoreType.DMA((2, n, chunks)),
-            pltpu.SemaphoreType.DMA((2, n, chunks, max(pairs - 1, 1))),
-            pltpu.SemaphoreType.DMA((2, n, chunks, max(pairs - 1, 1))),
-        ],
-        compiler_params=pltpu.CompilerParams(collective_id=number, has_side_effects=True),
-        cost_estimate=pl.CostEstimate(flops=100_000_000_000 // 4, bytes_accessed=sent, transcendentals=0),
+        scratch_shapes=ring_sems(n, pairs, chunks),
+        compiler_params=pltpu.CompilerParams(
+            collective_id=number, has_side_effects=True, vmem_limit_bytes=limit_of(first, second, out, out)
+        ),
+        cost_estimate=cost_of(sent),
         name=f"ring_gather_{number}",
     )(first, second)
+
+
+WEIGHT_CUTS = 4
+
+
+def project_kernel(sizes, groups, vision_hbm, key_hbm, value_hbm, gain_ref, keys_out, values_out, raw_out,
+                   columns_out, vision, key_weight, value_weight, own_keys, own_values, load_sem,
+                   push_send, push_recv, own_sem, mate_send, mate_recv, *sems):
+    pairs, n, heads_cut = sizes
+    samples, rows, width = vision.shape
+    columns = key_weight.shape[1]
+    head_dim = gain_ref.shape[1]
+    shard = columns_out.shape[-1]
+    lane, here, me = lax.axis_index("dp"), lax.axis_index("seq"), lax.axis_index("mp")
+    place = me % groups
+    depth = width // WEIGHT_CUTS
+    chunks = columns_out.shape[0]
+
+    loads = [pltpu.make_async_copy(vision_hbm, vision, load_sem.at[0])]
+    for at, (source, held) in enumerate(((key_hbm, key_weight), (value_hbm, value_weight))):
+        for cut in range(WEIGHT_CUTS):
+            span = pl.ds(cut * depth, depth)
+            loads.append(
+                pltpu.make_async_copy(
+                    source.at[span], held.at[span], load_sem.at[1 + at * WEIGHT_CUTS + cut]
+                )
+            )
+    for load in loads:
+        load.start()
+    shifts = range(1, pairs * n)
+    mates = [me - place + (place + shift) % groups for shift in range(1, groups)]
+    peers = [((lane + shift // n) % pairs, (here + shift % n) % n) for shift in shifts]
+    greet([{"dp": peer[0], "seq": peer[1]} for peer in peers] + [{"mp": mate} for mate in mates])
+    loads[0].wait()
+
+    which = [place] if groups > 1 else list(range(samples))
+    pushes, own_copies = [], []
+    for chunk in range(chunks):
+        for at, sample in enumerate(which):
+            def columns_of(pair, seat, chunk=chunk, sample=sample):
+                start = ((pair * chunks + chunk) * n + seat) * shard
+                return vision.at[sample, :, pl.ds(pl.multiple_of(start, shard), shard)]
+
+            target = columns_out.at[chunk, lane, sample, here]
+            copy = pltpu.make_async_copy(columns_of(lane, here), target, own_sem.at[chunk, at])
+            copy.start()
+            own_copies.append(copy)
+            for shift, peer in zip(shifts, peers):
+                copy = pltpu.make_async_remote_copy(
+                    src_ref=columns_of(*peer),
+                    dst_ref=target,
+                    send_sem=push_send.at[chunk, at, shift],
+                    recv_sem=push_recv.at[chunk, at, shift],
+                    device_id={"dp": peer[0], "seq": peer[1]},
+                    device_id_type=MESH,
+                )
+                copy.start()
+                pushes.append(copy)
+
+    def product(at, weight, cut, total):
+        loads[1 + at * WEIGHT_CUTS + cut].wait()
+        left = vision[:, :, cut * depth : (cut + 1) * depth].reshape(samples * rows, depth)
+        part = jnp.dot(left, weight[cut * depth : (cut + 1) * depth], preferred_element_type=F32)
+        return part if total is None else total + part
+
+    state = {}
+
+    def prepare(way):
+        if way == 0:
+            raw = None
+            for cut in range(WEIGHT_CUTS):
+                raw = product(0, key_weight, cut, raw)
+            for at in range(columns // head_dim):
+                span = slice(at * head_dim, (at + 1) * head_dim)
+                head = raw[:, span]
+                normed = (head * inverse_of(head) * gain_ref[...]).astype(BF16)
+                raw_out[:, :, span] = head.reshape(samples, rows, head_dim)
+                own_keys[:, :, span] = normed.reshape(samples, rows, head_dim)
+            state["values"] = product(1, value_weight, 0, None)
+            return
+        total = state["values"]
+        for cut in range(1, WEIGHT_CUTS):
+            total = product(1, value_weight, cut, total)
+        own_values[...] = total.astype(BF16).reshape(samples, rows, columns)
+
+    mate_copies = []
+
+    def forward():
+        for copy in own_copies:
+            copy.wait()
+        for copy in pushes:
+            copy.wait_recv()
+        for at, mate in enumerate(mates):
+            for chunk in range(chunks):
+                for pair in range(pairs):
+                    block = columns_out.at[chunk, pair, place]
+                    copy = pltpu.make_async_remote_copy(
+                        src_ref=block,
+                        dst_ref=block,
+                        send_sem=mate_send.at[at, chunk, pair],
+                        recv_sem=mate_recv.at[at, chunk, pair],
+                        device_id={"mp": mate},
+                        device_id_type=MESH,
+                    )
+                    copy.start()
+                    mate_copies.append(copy)
+
+    def idle():
+        pass
+
+    jobs = [idle] * 5 + [forward]
+    run_ring(n, 1, (own_keys, own_values), (keys_out, values_out), sems, prepare, jobs, kept=False)
+    for copy in pushes:
+        copy.wait_send()
+    for copy in mate_copies:
+        copy.wait_send()
+        copy.wait_recv()
+
+
+def project(sizes, vision, key_weight, value_weight, gain):
+    pairs, n, heads_cut = sizes
+    samples, rows, width = vision.shape
+    columns = key_weight.shape[1]
+    chunks = chunks_of(width, pairs, n)
+    shard = width // (pairs * chunks * n)
+    groups = samples if heads_cut % samples == 0 else 1
+    each = 1 if groups > 1 else samples
+    gathered = jax.ShapeDtypeStruct((samples, n, rows, columns), BF16)
+    raw = jax.ShapeDtypeStruct((samples, rows, columns), F32)
+    cut = jax.ShapeDtypeStruct((chunks, pairs, samples, n, rows, shard), BF16)
+    sent = 2 * samples * (n - 1) * rows * columns * 2 + size_of(cut)
+    dma = pltpu.SemaphoreType.DMA
+    own = pltpu.VMEM((samples, rows, columns), BF16)
+    return pl.pallas_call(
+        functools.partial(project_kernel, sizes, groups),
+        out_shape=(gathered, gathered, raw, cut),
+        in_specs=[pl.BlockSpec(memory_space=pl.ANY)] * 3 + [pl.BlockSpec(memory_space=VMEM)],
+        out_specs=(pl.BlockSpec(memory_space=VMEM),) * 4,
+        scratch_shapes=[
+            pltpu.VMEM(vision.shape, BF16),
+            pltpu.VMEM(key_weight.shape, BF16),
+            pltpu.VMEM(value_weight.shape, BF16),
+            own,
+            own,
+            dma((1 + 2 * WEIGHT_CUTS,)),
+            dma((chunks, each, pairs * n)),
+            dma((chunks, each, pairs * n)),
+            dma((chunks, each)),
+            dma((max(groups - 1, 1), chunks, pairs)),
+            dma((max(groups - 1, 1), chunks, pairs)),
+        ]
+        + ring_sems(n, 1, samples),
+        compiler_params=pltpu.CompilerParams(
+            collective_id=1,
+            has_side_effects=True,
+            vmem_limit_bytes=limit_of(vision, key_weight, value_weight, gathered, gathered, raw, raw, cut),
+        ),
+        cost_estimate=cost_of(sent),
+        name="project_gather",
+    )(vision, key_weight, value_weight, gain)
+
+
+def vision_kernel(sizes, tile, key_ref, value_ref, key_hbm, value_hbm, key_out, value_out, vision_out,
+                  key_weight, value_weight, leaving, arrived, total, load_sem, leave_sem, arrive_sem, *sems):
+    pairs, n, heads_cut = sizes
+    me = lax.axis_index("mp")
+    loads = [
+        pltpu.make_async_copy(key_hbm, key_weight, load_sem.at[0]),
+        pltpu.make_async_copy(value_hbm, value_weight, load_sem.at[1]),
+    ]
+    for load in loads:
+        load.start()
+    mates = [(me + shift) % heads_cut for shift in range(1, heads_cut)]
+    greet_ring(n, pairs, [{"mp": mate} for mate in mates])
+    share = total.shape[1]
+    columns = key_ref.shape[-1]
+    tiles = share // tile
+    copies = []
+
+    def compute(owner, at, store):
+        span = pl.ds(pl.multiple_of(owner * share + at * tile, tile), tile)
+        part = None
+        for ref, weight in ((key_ref, key_weight), (value_ref, value_weight)):
+            left = ref[...].reshape(total.shape[0], columns)
+            term = lax.dot_general(
+                left, weight[span, :], (((1,), (1,)), ((), ())), preferred_element_type=F32
+            )
+            part = term if part is None else part + term
+        store(part)
+
+    def load_all():
+        for load in loads:
+            load.wait()
+
+    def leave(at):
+        copy = pltpu.make_async_remote_copy(
+            src_ref=leaving.at[at],
+            dst_ref=arrived.at[at],
+            send_sem=leave_sem.at[at],
+            recv_sem=arrive_sem.at[at],
+            device_id={"mp": mates[at]},
+            device_id_type=MESH,
+        )
+        copy.start()
+        copies.append(copy)
+
+    jobs = [load_all]
+    waiting = None
+    for turn, owner in enumerate(mates + [me]):
+        for at in range(tiles):
+            span = slice(at * tile, (at + 1) * tile)
+
+            def job(turn=turn, owner=owner, at=at, span=span, due=waiting):
+                def store(part):
+                    if turn < len(mates):
+                        leaving[turn, :, span] = part.astype(BF16)
+                    else:
+                        total[:, span] = part
+
+                compute(owner, at, store)
+                if due is not None:
+                    leave(due)
+
+            jobs.append(job)
+            waiting = None
+        waiting = turn
+    run_ring(n, pairs, (key_ref, value_ref), (key_out, value_out), sems, None, jobs)
+    result = total[...]
+    for at, copy in enumerate(copies):
+        copy.wait()
+        result = result + arrived[at].astype(F32)
+    vision_out[...] = result.astype(BF16)
+
+
+def vision_gather(sizes, key_grad, value_grad, key_weight, value_weight):
+    pairs, n, heads_cut = sizes
+    samples, rows, columns = key_grad.shape
+    share = key_weight.shape[0] // heads_cut
+    tile = 512 if share % 512 == 0 else share
+    out = jax.ShapeDtypeStruct((pairs, samples, n, rows, columns), BF16)
+    vision = jax.ShapeDtypeStruct((samples * rows, share), BF16)
+    moved = jax.ShapeDtypeStruct((max(heads_cut - 1, 1), samples * rows, share), BF16)
+    sent = 2 * samples * (n - 1) * rows * columns * 2
+    dma = pltpu.SemaphoreType.DMA
+    total = jax.ShapeDtypeStruct((samples * rows, share), F32)
+    return pl.pallas_call(
+        functools.partial(vision_kernel, sizes, tile),
+        out_shape=(out, out, vision),
+        in_specs=[pl.BlockSpec(memory_space=VMEM)] * 2 + [pl.BlockSpec(memory_space=pl.ANY)] * 2,
+        out_specs=(pl.BlockSpec(memory_space=VMEM),) * 3,
+        scratch_shapes=[
+            pltpu.VMEM(key_weight.shape, BF16),
+            pltpu.VMEM(value_weight.shape, BF16),
+            pltpu.VMEM(moved.shape, BF16),
+            pltpu.VMEM(moved.shape, BF16),
+            pltpu.VMEM(total.shape, F32),
+            dma((2,)),
+            dma((max(heads_cut - 1, 1),)),
+            dma((max(heads_cut - 1, 1),)),
+        ]
+        + ring_sems(n, pairs, samples),
+        compiler_params=pltpu.CompilerParams(
+            collective_id=3,
+            has_side_effects=True,
+            vmem_limit_bytes=limit_of(
+                key_grad, value_grad, key_weight, value_weight, moved, moved, total, total, out, out, vision
+            ),
+        ),
+        cost_estimate=cost_of(sent),
+        name="vision_gather",
+    )(key_grad, value_grad, key_weight, value_weight)
 
 
 def scatter_kernel(n, head_dim, key_ref, value_ref, raw_ref, gain_ref, key_out, value_out, *scratch):
@@ -195,18 +511,14 @@
             pltpu.SemaphoreType.DMA((2, n - 1, chunks)),
             pltpu.SemaphoreType.DMA((2, n - 1, chunks)),
         ],
-        compiler_params=pltpu.CompilerParams(collective_id=number, has_side_effects=True),
-        cost_estimate=pl.CostEstimate(flops=100_000_000_000 // 4, bytes_accessed=sent, transcendentals=0),
+        compiler_params=pltpu.CompilerParams(
+            collective_id=number,
+            has_side_effects=True,
+            vmem_limit_bytes=limit_of(key_part, value_part, key_part, value_part, key_raw, out, out),
+        ),
+        cost_estimate=cost_of(sent),
         name="ring_scatter",
     )(key_part, value_part, key_raw, gain)
-
-
-def norm_kernel(head_dim, raw_ref, gain_ref, out_ref):
-    gain = gain_ref[...]
-    for at in range(raw_ref.shape[-1] // head_dim):
-        cut = slice(at * head_dim, (at + 1) * head_dim)
-        raw = raw_ref[:, :, cut]
-        out_ref[:, :, cut] = (raw * inverse_of(raw) * gain).astype(BF16)
 
 
 def attention_kernel(group, tile_tokens, tiles_ref, query_ref, grad_ref, key_ref, value_ref, gain_ref,
@@ -280,32 +592,18 @@
 
 def local(sizes, queries, vision, key_weight, value_weight, query_gain, key_gain, out_grad, tile_count):
     pairs, n, heads_cut = sizes
-    head_dim = query_gain.shape[0]
     samples, rows, model_width = vision.shape
     columns = key_weight.shape[1]
-    flat_vision = vision.reshape(samples * rows, model_width)
-
-    shard = model_width // (pairs * CHUNKS * n)
-    cut = flat_vision.reshape(samples * rows, pairs, CHUNKS, n, shard)
-    cut = cut.transpose(1, 3, 0, 2, 4).reshape(pairs * n, samples * rows, CHUNKS * shard)
-    column_vision = lax.all_to_all(cut, ("dp", "seq"), split_axis=0, concat_axis=0, tiled=True)
-    column_vision = column_vision.reshape(pairs, n, samples, rows, CHUNKS * shard)
-    column_vision = column_vision.transpose(0, 2, 1, 3, 4).reshape(-1, CHUNKS * shard)
-
-    key_raw = jnp.dot(flat_vision, key_weight, preferred_element_type=F32)
-    key_raw = key_raw.reshape(samples, rows, columns)
-    own_values = jnp.dot(flat_vision, value_weight, preferred_element_type=F32).astype(BF16)
-    own_values = own_values.reshape(samples, rows, columns)
-    own_keys = pl.pallas_call(
-        functools.partial(norm_kernel, head_dim),
-        out_shape=jax.ShapeDtypeStruct(key_raw.shape, BF16),
-        name="key_norm",
-    )(key_raw, key_gain[None])
-    keys_all, values_all = ring_gather(own_keys, own_values, n, 1, 1)
-    keys_all = keys_all.reshape(samples, n * rows, columns)
-    values_all = values_all.reshape(samples, n * rows, columns)
+    keys_all, values_all, key_raw, column_vision = project(
+        sizes, vision, key_weight, value_weight, key_gain[None]
+    )
     query_grad, key_part, value_part = attention(
-        tile_count, queries, out_grad, keys_all, values_all, query_gain[None]
+        tile_count,
+        queries,
+        out_grad,
+        keys_all.reshape(samples, n * rows, columns),
+        values_all.reshape(samples, n * rows, columns),
+        query_gain[None],
     )
     key_grad, value_grad = ring_scatter(
         key_part.reshape(samples, n, rows, columns),
@@ -314,34 +612,21 @@
         key_gain[None],
         2,
     )
-
-    share = model_width // heads_cut
-    vision_part = jnp.einsum(
-        "rc,dc->rd", key_grad.reshape(samples * rows, columns), key_weight, preferred_element_type=F32
-    ) + jnp.einsum(
-        "rc,dc->rd", value_grad.reshape(samples * rows, columns), value_weight, preferred_element_type=F32
-    )
-    me = lax.axis_index("mp")
-    total = lax.dynamic_slice_in_dim(vision_part, me * share, share, axis=1)
-    for shift in range(1, heads_cut):
-        leaving = lax.dynamic_slice_in_dim(
-            vision_part, lax.rem(me + shift, heads_cut) * share, share, axis=1
-        ).astype(BF16)
-        arrived = lax.ppermute(leaving, "mp", [(at, (at + shift) % heads_cut) for at in range(heads_cut)])
-        total = total + arrived.astype(F32)
-    vision_grad = total.astype(BF16).reshape(samples, rows, share)
-
-    every_key, every_value = ring_gather(key_grad, value_grad, n, pairs, 3)
+    every_key, every_value, vision_grad = vision_gather(
+        sizes, key_grad, value_grad, key_weight, value_weight
+    )
+    tokens = pairs * samples * n * rows
+    column_vision = column_vision.reshape(column_vision.shape[0], tokens, -1)
     outs = []
     for every in (every_key, every_value):
         grad = jnp.einsum(
-            "td,tc->dc", column_vision, every.reshape(-1, columns), preferred_element_type=F32
+            "ktd,tc->kdc", column_vision, every.reshape(tokens, columns), preferred_element_type=F32
         )
-        outs.append(grad.astype(BF16).reshape(CHUNKS, shard, columns))
+        outs.append(grad.astype(BF16))
     key_rows, value_rows = ring_gather(outs[0], outs[1], n, pairs, 4)
     return (
         query_grad,
-        vision_grad,
+        vision_grad.reshape(samples, rows, -1),
         key_rows.reshape(model_width, columns).astype(F32),
         value_rows.reshape(model_width, columns).astype(F32),
     )

time: 245 us -> 201 us (0.82)
  matrix products: 21.8 us -> 1.71 us
  Pallas kernels: 189 us -> 178 us
  starting transfers between devices: 9.01 us -> 0 us
  other arithmetic: 14.1 us -> 10.8 us
    pallas_call x3 -> x1, Pallas kernels: 137 us -> 44.6 us  [ring_gather(): pl.pallas_call(functools.partial(gather_kernel, n, pairs), out_shape=(out...]
    pallas_call x1 -> x2, Pallas kernels: 1.81 us -> 84.4 us  [the longest x1 51.5 us: project(): pl.pallas_call(functools.partial(project_kernel, sizes, groups), out_shap...]
    dot_general x6 -> x2, matrix products: 21.8 us -> 1.71 us  [local(): jnp.einsum('ktd,tc->kdc', column_vision, every.reshape(tokens, columns),...]
    all_to_all x1 -> x0, starting transfers between devices: 7.43 us -> none  [local(): lax.all_to_all(cut, ('dp', 'seq'), split_axis=0, concat_axis=0, tiled=True)]
    unnamed x25 -> x27, local copies, waits for them, and re-layouts: 6.54 us -> 10.2 us
  transfers between devices with their start and end apart: 2 -> 0, of which waited for: 0 -> 0; matrix products, arithmetic and copies ran while one was open for 7% -> 0% of each run, Pallas kernels for 57% -> 0%
where the time goes in v2:
time: 201 us
  Pallas kernels  178 us (89%)
  other arithmetic  10.8 us (5%)
  local copies, waits for them, and re-layouts  10.2 us (5%)
    pallas_call x1, Pallas kernels, project(): pl.pallas_call(functools.partial(project_kernel, sizes, groups), out_shap...  51.5 us
    pallas_call x1, Pallas kernels, ring_gather(): pl.pallas_call(functools.partial(gather_kernel, n, pairs), out_shape=(out...  44.6 us
    pallas_call x1, Pallas kernels, vision_gather(): pl.pallas_call(functools.partial(vision_kernel, sizes, tile), out_shape=(...  32.9 us
    pallas_call x1, Pallas kernels, ring_scatter(): pl.pallas_call(functools.partial(scatter_kernel, n, gain.shape[1]), out_s...  30.4 us
    pallas_call x1, Pallas kernels, attention(): pl.pallas_call(functools.partial(attention_kernel, group, tokens // MAX_T...  18.2 us
    convert_element_type x1, other arithmetic, local(): value_rows.reshape(model_width, columns).astype(F32)  10.8 us
    unnamed x27, local copies, waits for them, and re-layouts  10.2 us

profile of v2, /device:TPU:0, one launch (start us, length us, event | category | flops | bytes accessed | tf_op | source)
XLA Modules:
  0.0 201.0 jit_solution(1730738271120670004)
XLA Ops:
  0.6 0.0 copy-start.1
  0.6 2.2 %copy-done.1 = bf16[4096,512]{1,0:T(8,128)(2,1)S(1)} copy-done((bf16[4096,512]{1,0:T(8,128)(2,1)S(1)}, bf16[4096,512]{1,0:T(8,128)(2,1)}, u32[]{:S(2)}) %copy-start.1) | copy-done | bytes 4194328
  2.8 0.0 copy-start.3
  2.8 2.2 %copy-done.3 = bf16[4096,512]{1,0:T(8,128)(2,1)S(1)} copy-done((bf16[4096,512]{1,0:T(8,128)(2,1)S(1)}, bf16[4096,512]{1,0:T(8,128)(2,1)}, u32[]{:S(2)}) %copy-start.3) | copy-done | bytes 4194328
  5.0 0.0 copy-start.5
  5.0 1.3 copy-done.5
  6.3 0.0 copy-start.10
  6.3 0.7 copy-done.10
  7.0 0.0 copy-start.6
  7.0 0.0 copy-start.7
  7.0 0.0 copy-start.8
  7.0 51.5 %project_gather.1 = (bf16[2,8,80,512]{3,2,1,0:T(8,128)(2,1)S(1)}, bf16[2,8,80,512]{3,2,1,0:T(8,128)(2,1)S(1)}, f32[2,80,512]{2,1,0:T(8,128)S(1)}, bf16[2,2,2,8,80,128]{5,4,3,2,1,0:T(8,128)(2,1)S(1)}) custom-call(bf16[2,80,4096]{2,1,0:T(8,128)(2,1)S(1)} %copy-done.5, bf16[4096,512]{1,0:T(8,128)(2,1)S(1)} %copy-done.1, bf16[4096,512]{1,0:T(8,128)(2,1)S(1)} %copy-done.3, ...), custom_call_target="tpu_custom_call" | custom-call | flops 24999999488 | bytes 3604480 | tf_op jit(solution)/shard_map/project_gather/pallas_call | solution.py:306
  58.5 0.0 copy-start.12
  58.5 1.0 copy-done.12
  59.5 0.0 copy-done.6
  59.5 0.0 copy-done.7
  59.5 0.0 copy-done.8
  59.5 0.0 copy-done.9
  59.5 0.0 copy-start.11
  59.5 18.2 %attention.1 = (bf16[2,128,2048]{2,1,0:T(8,128)(2,1)}, bf16[2,640,512]{2,1,0:T(8,128)(2,1)S(1)}, bf16[2,640,512]{2,1,0:T(8,128)(2,1)S(1)}) custom-call(s32[2]{0:T(128)S(1)} %copy-done.8, bf16[2,128,2048]{2,1,0:T(8,128)(2,1)S(1)} %copy-done.6, bf16[2,128,2048]{2,1,0:T(8,128)(2,1)S(1)} %copy-done.7, bf16[2,640,512]{2,1,0:T(8,128)(2,1)S(1)} %bitcast.59, ...), custom_call_target="tpu_custom_call" | custom-call | flops 3355443200 | bytes 8000000 | tf_op jit(solution)/shard_map/attention/pallas_call | solution.py:574
  77.7 0.0 copy-done.11
  77.7 30.4 %ring_scatter.1 = (bf16[2,80,512]{2,1,0:T(8,128)(2,1)S(1)}, bf16[2,80,512]{2,1,0:T(8,128)(2,1)S(1)}) custom-call(bf16[2,8,80,512]{3,2,1,0:T(8,128)(2,1)S(1)} %bitcast.57, bf16[2,8,80,512]{3,2,1,0:T(8,128)(2,1)S(1)} %bitcast.58, f32[2,80,512]{2,1,0:T(8,128)S(1)} %get-tuple-element.23.raw_ref, f32[1,128]{1,0:T(1,128)S(1)} %bitcast.56), custom_call_target="tpu_custom_call" | custom-call | flops 24999999488 | bytes 2293760 | tf_op jit(solution)/shard_map/ring_scatter/pallas_call | solution.py:504
  108.1 0.0 copy-done.2
  108.1 0.0 copy-done.4
  108.1 32.9 %vision_gather.1 = (bf16[2,2,8,80,512]{4,3,2,1,0:T(8,128)(2,1)S(1)}, bf16[2,2,8,80,512]{4,3,2,1,0:T(8,128)(2,1)S(1)}, bf16[160,2048]{1,0:T(8,128)(2,1)S(1)}) custom-call(bf16[2,80,512]{2,1,0:T(8,128)(2,1)S(1)} %get-tuple-element.24.key_ref, bf16[2,80,512]{2,1,0:T(8,128)(2,1)S(1)} %get-tuple-element.25.value_ref, bf16[4096,512]{1,0:T(8,128)(2,1)S(1)} %copy-done.2, ...), custom_call_target="tpu_custom_call" | custom-call | flops 24999999488 | bytes 2293760 | tf_op jit(solution)/shard_map/vision_gather/pallas_call | solution.py:418
  141.1 0.9 fusion.13.first_ref
  142.0 0.9 fusion.10.second_ref
  142.8 44.6 %ring_gather_4.1 = (bf16[2,2,8,128,512]{4,3,2,1,0:T(8,128)(2,1)S(1)}, bf16[2,2,8,128,512]{4,3,2,1,0:T(8,128)(2,1)S(1)}) custom-call(bf16[2,128,512]{2,1,0:T(8,128)(2,1)S(1)} %fusion.13.first_ref, bf16[2,128,512]{2,1,0:T(8,128)(2,1)S(1)} %fusion.10.second_ref), custom_call_target="tpu_custom_call" | custom-call | flops 24999999488 | bytes 3670016 | tf_op jit(solution)/shard_map/ring_gather_4/pallas_call | solution.py:161
  187.5 0.0 copy-start
  187.5 1.9 copy-done
  189.4 10.8 %bitcast_convert_fusion = (f32[4096,512]{1,0:T(8,128)}, f32[4096,512]{1,0:T(8,128)}) fusion(bf16[2,2,8,128,512]{4,3,2,1,0:T(8,128)(2,1)} %copy-done, bf16[2,2,8,128,512]{4,3,2,1,0:T(8,128)(2,1)S(1)} %get-tuple-element.30), kind=kLoop, calls=%fused_computation | loop fusion | flops 4194304 | bytes 25165824 | tf_op jit(solution)/shard_map/convert_element_type | solution.py:631
  200.2 0.8 copy.18
  (3 shorter events, 0.0 us)
Async XLA Ops:
  0.6 2.2 %copy-start.1 = (bf16[4096,512]{1,0:T(8,128)(2,1)S(1)}, bf16[4096,512]{1,0:T(8,128)(2,1)}, u32[]{:S(2)}) copy-start(bf16[4096,512]{1,0:T(8,128)(2,1)} %key_hbm.3) | copy-start | bytes 12582916
  2.8 2.2 %copy-start.3 = (bf16[4096,512]{1,0:T(8,128)(2,1)S(1)}, bf16[4096,512]{1,0:T(8,128)(2,1)}, u32[]{:S(2)}) copy-start(bf16[4096,512]{1,0:T(8,128)(2,1)} %value_hbm.3) | copy-start | bytes 12582916
  5.0 1.3 copy-start.5
  6.3 0.7 copy-start.10
  7.0 52.5 %copy-start.6 = (bf16[2,128,2048]{2,1,0:T(8,128)(2,1)S(1)}, bf16[2,128,2048]{2,1,0:T(8,128)(2,1)}, u32[]{:S(2)}) copy-start(bf16[2,128,2048]{2,1,0:T(8,128)(2,1)} %query_ref.1) | copy-start | bytes 3145732
  7.0 52.5 %copy-start.7 = (bf16[2,128,2048]{2,1,0:T(8,128)(2,1)S(1)}, bf16[2,128,2048]{2,1,0:T(8,128)(2,1)}, u32[]{:S(2)}) copy-start(bf16[2,128,2048]{2,1,0:T(8,128)(2,1)} %grad_ref.1) | copy-start | bytes 3145732
  7.0 52.5 %copy-start.8 = (s32[2]{0:T(128)S(1)}, s32[2]{0:T(128)}, u32[]{:S(2)}) copy-start(s32[2]{0:T(128)} %tiles_ref.1) | copy-start | bytes 28
  7.0 52.5 %copy-start.9 = (f32[128]{0:T(128)S(1)}, f32[128]{0:T(128)}, u32[]{:S(2)}) copy-start(f32[128]{0:T(128)} %param.12) | copy-start | bytes 1540
  58.5 1.1 copy-start.12
  59.5 18.2 %copy-start.11 = (f32[128]{0:T(128)S(1)}, f32[128]{0:T(128)}, u32[]{:S(2)}) copy-start(f32[128]{0:T(128)} %param.13) | copy-start | bytes 1540
  77.7 30.4 %copy-start.2 = (bf16[4096,512]{1,0:T(8,128)(2,1)S(1)}, bf16[4096,512]{1,0:T(8,128)(2,1)}, u32[]{:S(2)}) copy-start(bf16[4096,512]{1,0:T(8,128)(2,1)} %key_hbm.3) | copy-start | bytes 12582916
  77.7 30.4 %copy-start.4 = (bf16[4096,512]{1,0:T(8,128)(2,1)S(1)}, bf16[4096,512]{1,0:T(8,128)(2,1)}, u32[]{:S(2)}) copy-start(bf16[4096,512]{1,0:T(8,128)(2,1)} %value_hbm.3) | copy-start | bytes 12582916
  187.5 2.0 copy-start

commit v3 on v2

--- a/solution.py
+++ b/solution.py
@@ -175,18 +175,13 @@
 WEIGHT_CUTS = 4
 
 
-def project_kernel(sizes, groups, vision_hbm, key_hbm, value_hbm, gain_ref, keys_out, values_out, raw_out,
-                   columns_out, vision, key_weight, value_weight, own_keys, own_values, load_sem,
-                   push_send, push_recv, own_sem, mate_send, mate_recv, *sems):
+def project_kernel(sizes, vision_hbm, key_hbm, value_hbm, gain_ref, keys_out, values_out, raw_out,
+                   vision, key_weight, value_weight, own_keys, own_values, load_sem, *sems):
     pairs, n, heads_cut = sizes
     samples, rows, width = vision.shape
     columns = key_weight.shape[1]
     head_dim = gain_ref.shape[1]
-    shard = columns_out.shape[-1]
-    lane, here, me = lax.axis_index("dp"), lax.axis_index("seq"), lax.axis_index("mp")
-    place = me % groups
     depth = width // WEIGHT_CUTS
-    chunks = columns_out.shape[0]
 
     loads = [pltpu.make_async_copy(vision_hbm, vision, load_sem.at[0])]
     for at, (source, held) in enumerate(((key_hbm, key_weight), (value_hbm, value_weight))):
@@ -199,35 +194,8 @@
             )
     for load in loads:
         load.start()
-    shifts = range(1, pairs * n)
-    mates = [me - place + (place + shift) % groups for shift in range(1, groups)]
-    peers = [((lane + shift // n) % pairs, (here + shift % n) % n) for shift in shifts]
-    greet([{"dp": peer[0], "seq": peer[1]} for peer in peers] + [{"mp": mate} for mate in mates])
+    greet_ring(n, 1)
     loads[0].wait()
-
-    which = [place] if groups > 1 else list(range(samples))
-    pushes, own_copies = [], []
-    for chunk in range(chunks):
-        for at, sample in enumerate(which):
-            def columns_of(pair, seat, chunk=chunk, sample=sample):
-                start = ((pair * chunks + chunk) * n + seat) * shard
-                return vision.at[sample, :, pl.ds(pl.multiple_of(start, shard), shard)]
-
-            target = columns_out.at[chunk, lane, sample, here]
-            copy = pltpu.make_async_copy(columns_of(lane, here), target, own_sem.at[chunk, at])
-            copy.start()
-            own_copies.append(copy)
-            for shift, peer in zip(shifts, peers):
-                copy = pltpu.make_async_remote_copy(
-                    src_ref=columns_of(*peer),
-                    dst_ref=target,
-                    send_sem=push_send.at[chunk, at, shift],
-                    recv_sem=push_recv.at[chunk, at, shift],
-                    device_id={"dp": peer[0], "seq": peer[1]},
-                    device_id_type=MESH,
-                )
-                copy.start()
-                pushes.append(copy)
 
     def product(at, weight, cut, total):
         loads[1 + at * WEIGHT_CUTS + cut].wait()
@@ -255,59 +223,23 @@
             total = product(1, value_weight, cut, total)
         own_values[...] = total.astype(BF16).reshape(samples, rows, columns)
 
-    mate_copies = []
-
-    def forward():
-        for copy in own_copies:
-            copy.wait()
-        for copy in pushes:
-            copy.wait_recv()
-        for at, mate in enumerate(mates):
-            for chunk in range(chunks):
-                for pair in range(pairs):
-                    block = columns_out.at[chunk, pair, place]
-                    copy = pltpu.make_async_remote_copy(
-                        src_ref=block,
-                        dst_ref=block,
-                        send_sem=mate_send.at[at, chunk, pair],
-                        recv_sem=mate_recv.at[at, chunk, pair],
-                        device_id={"mp": mate},
-                        device_id_type=MESH,
-                    )
-                    copy.start()
-                    mate_copies.append(copy)
-
-    def idle():
-        pass
-
-    jobs = [idle] * 5 + [forward]
-    run_ring(n, 1, (own_keys, own_values), (keys_out, values_out), sems, prepare, jobs, kept=False)
-    for copy in pushes:
-        copy.wait_send()
-    for copy in mate_copies:
-        copy.wait_send()
-        copy.wait_recv()
+    run_ring(n, 1, (own_keys, own_values), (keys_out, values_out), sems, prepare, kept=False)
 
 
 def project(sizes, vision, key_weight, value_weight, gain):
     pairs, n, heads_cut = sizes
     samples, rows, width = vision.shape
     columns = key_weight.shape[1]
-    chunks = chunks_of(width, pairs, n)
-    shard = width // (pairs * chunks * n)
-    groups = samples if heads_cut % samples == 0 else 1
-    each = 1 if groups > 1 else samples
     gathered = jax.ShapeDtypeStruct((samples, n, rows, columns), BF16)
     raw = jax.ShapeDtypeStruct((samples, rows, columns), F32)
-    cut = jax.ShapeDtypeStruct((chunks, pairs, samples, n, rows, shard), BF16)
-    sent = 2 * samples * (n - 1) * rows * columns * 2 + size_of(cut)
+    sent = 2 * samples * (n - 1) * rows * columns * 2
     dma = pltpu.SemaphoreType.DMA
     own = pltpu.VMEM((samples, rows, columns), BF16)
     return pl.pallas_call(
-        functools.partial(project_kernel, sizes, groups),
-        out_shape=(gathered, gathered, raw, cut),
-        in_specs=[pl.BlockSpec(memory_space=pl.ANY)] * 3 + [pl.BlockSpec(memory_space=VMEM)],
-        out_specs=(pl.BlockSpec(memory_space=VMEM),) * 4,
+        functools.partial(project_kernel, sizes),
+        out_shape=(gathered, gathered, raw),
+        in_specs=[pl.BlockSpec(memory_space=pltpu.HBM)] * 3 + [pl.BlockSpec(memory_space=VMEM)],
+        out_specs=(pl.BlockSpec(memory_space=VMEM),) * 3,
         scratch_shapes=[
             pltpu.VMEM(vision.shape, BF16),
             pltpu.VMEM(key_weight.shape, BF16),
@@ -315,17 +247,12 @@
             own,
             own,
             dma((1 + 2 * WEIGHT_CUTS,)),
-            dma((chunks, each, pairs * n)),
-            dma((chunks, each, pairs * n)),
-            dma((chunks, each)),
-            dma((max(groups - 1, 1), chunks, pairs)),
-            dma((max(groups - 1, 1), chunks, pairs)),
         ]
         + ring_sems(n, 1, samples),
         compiler_params=pltpu.CompilerParams(
             collective_id=1,
             has_side_effects=True,
-            vmem_limit_bytes=limit_of(vision, key_weight, value_weight, gathered, gathered, raw, raw, cut),
+            vmem_limit_bytes=60 * 1024 * 1024,
         ),
         cost_estimate=cost_of(sent),
         name="project_gather",
@@ -418,7 +345,7 @@
     return pl.pallas_call(
         functools.partial(vision_kernel, sizes, tile),
         out_shape=(out, out, vision),
-        in_specs=[pl.BlockSpec(memory_space=VMEM)] * 2 + [pl.BlockSpec(memory_space=pl.ANY)] * 2,
+        in_specs=[pl.BlockSpec(memory_space=VMEM)] * 2 + [pl.BlockSpec(memory_space=pltpu.HBM)] * 2,
         out_specs=(pl.BlockSpec(memory_space=VMEM),) * 3,
         scratch_shapes=[
             pltpu.VMEM(key_weight.shape, BF16),
@@ -443,12 +370,15 @@
     )(key_grad, value_grad, key_weight, value_weight)
 
 
-def scatter_kernel(n, head_dim, key_ref, value_ref, raw_ref, gain_ref, key_out, value_out, *scratch):
-    held, send_sem, recv_sem = scratch
+def scatter_kernel(n, groups, head_dim, key_ref, value_ref, raw_ref, gain_ref, half_ref, key_out, value_out,
+                   columns_out, held, send_sem, recv_sem, own_sem, mate_send, mate_recv):
     parts = (key_ref, value_ref)
     here, place, nexts = ring(n)
     chunks = key_ref.shape[0]
-    greet([{"seq": nexts[0]}, {"seq": nexts[1]}])
+    me = lax.axis_index("mp")
+    seat = me % groups
+    mates = [me - seat + (seat + shift) % groups for shift in range(1, groups)]
+    greet([{"seq": nexts[0]}, {"seq": nexts[1]}] + [{"mp": mate} for mate in mates])
 
     def copy_of(way, step, chunk, block):
         return pltpu.make_async_remote_copy(
@@ -471,6 +401,26 @@
             copy = copy_of(way, 0, chunk, parts[way].at[chunk, dest_of(way, 0)])
             copy.start()
             copies[way, 0, chunk] = copy
+    moved = []
+    for cut in range(half_ref.shape[0]):
+        for pair in range(half_ref.shape[1]):
+            for at in range(half_ref.shape[2]):
+                block = half_ref.at[cut, pair, at]
+                target = columns_out.at[cut, pair, seat if groups > 1 else at]
+                moved.append(pltpu.make_async_copy(block, target, own_sem.at[cut, pair, at]))
+                for turn, mate in enumerate(mates):
+                    moved.append(
+                        pltpu.make_async_remote_copy(
+                            src_ref=block,
+                            dst_ref=target,
+                            send_sem=mate_send.at[cut, pair, turn],
+                            recv_sem=mate_recv.at[cut, pair, turn],
+                            device_id={"mp": mate},
+                            device_id_type=MESH,
+                        )
+                    )
+    for copy in moved:
+        copy.start()
     for step in range(1, n):
         for chunk in range(chunks):
             for way in range(2):
@@ -495,34 +445,84 @@
                     copies[way, step, chunk] = copy
     for copy in copies.values():
         copy.wait_send()
-
-
-def ring_scatter(key_part, value_part, key_raw, gain, number):
+    for copy in moved:
+        copy.wait()
+
+
+def ring_scatter(sizes, key_part, value_part, key_raw, gain, half, number):
     chunks, n, rows, columns = key_part.shape
+    groups = chunks if sizes[2] % chunks == 0 else 1
+    cuts, pairs, each = half.shape[:3]
+    full = jax.ShapeDtypeStruct((cuts, pairs, chunks) + half.shape[3:], BF16)
+    dma = pltpu.SemaphoreType.DMA
     out = jax.ShapeDtypeStruct((chunks, rows, columns), BF16)
     sent = 2 * chunks * (n - 1) * rows * columns * 2
     return pl.pallas_call(
-        functools.partial(scatter_kernel, n, gain.shape[1]),
-        out_shape=(out, out),
-        in_specs=[pl.BlockSpec(memory_space=VMEM)] * 4,
-        out_specs=(pl.BlockSpec(memory_space=VMEM),) * 2,
+        functools.partial(scatter_kernel, n, groups, gain.shape[1]),
+        out_shape=(out, out, full),
+        in_specs=[pl.BlockSpec(memory_space=VMEM)] * 5,
+        out_specs=(pl.BlockSpec(memory_space=VMEM),) * 3,
         scratch_shapes=[
             pltpu.VMEM((2, n - 1, chunks, rows, columns), BF16),
-            pltpu.SemaphoreType.DMA((2, n - 1, chunks)),
-            pltpu.SemaphoreType.DMA((2, n - 1, chunks)),
+            dma((2, n - 1, chunks)),
+            dma((2, n - 1, chunks)),
+            dma((cuts, pairs, each)),
+            dma((cuts, pairs, max(groups - 1, 1))),
+            dma((cuts, pairs, max(groups - 1, 1))),
         ],
         compiler_params=pltpu.CompilerParams(
             collective_id=number,
             has_side_effects=True,
-            vmem_limit_bytes=limit_of(key_part, value_part, key_part, value_part, key_raw, out, out),
+            vmem_limit_bytes=limit_of(key_part, value_part, key_part, value_part, key_raw, out, out, half, full),
         ),
         cost_estimate=cost_of(sent),
         name="ring_scatter",
-    )(key_part, value_part, key_raw, gain)
-
-
-def attention_kernel(group, tile_tokens, tiles_ref, query_ref, grad_ref, key_ref, value_ref, gain_ref,
-                     query_out, key_out, value_out):
+    )(key_part, value_part, key_raw, gain, half)
+
+
+def exchange(sizes, groups, vision, columns_out, push_send, push_recv, own_sem):
+    pairs, n, _ = sizes
+    chunks, each, shard = columns_out.shape[0], columns_out.shape[2], columns_out.shape[-1]
+    lane, here, me = lax.axis_index("dp"), lax.axis_index("seq"), lax.axis_index("mp")
+    peers = [((lane + shift // n) % pairs, (here + shift % n) % n) for shift in range(1, pairs * n)]
+    own, pushes = [], []
+    for chunk in range(chunks):
+        for at in range(each):
+            sample = me % groups if groups > 1 else at
+
+            def columns_of(pair, seat, chunk=chunk, sample=sample):
+                start = ((pair * chunks + chunk) * n + seat) * shard
+                return vision.at[sample, :, pl.ds(pl.multiple_of(start, shard), shard)]
+
+            target = columns_out.at[chunk, lane, at, here]
+            own.append(pltpu.make_async_copy(columns_of(lane, here), target, own_sem.at[chunk, at]))
+            for shift, peer in enumerate(peers):
+                pushes.append(
+                    pltpu.make_async_remote_copy(
+                        src_ref=columns_of(*peer),
+                        dst_ref=target,
+                        send_sem=push_send.at[chunk, at, shift],
+                        recv_sem=push_recv.at[chunk, at, shift],
+                        device_id={"dp": peer[0], "seq": peer[1]},
+                        device_id_type=MESH,
+                    )
+                )
+    return peers, own + pushes
+
+
+def attention_kernel(sizes, groups, group, tile_tokens, tiles_ref, query_ref, grad_ref, key_ref, value_ref,
+                     gain_ref, vision, query_out, key_out, value_out, columns_out, *sems):
+    at_sample, at_head = pl.program_id(0), pl.program_id(1)
+    heads = pl.num_programs(1)
+    turn = at_sample * heads + at_head
+
+    @pl.when(turn == 0)
+    def _():
+        peers, copies = exchange(sizes, groups, vision, columns_out, *sems)
+        greet([{"dp": peer[0], "seq": peer[1]} for peer in peers])
+        for copy in copies:
+            copy.start()
+
     text_rows = query_ref.shape[1]
     head_dim = key_ref.shape[2]
     scale = head_dim ** (-0.5)
@@ -560,8 +560,15 @@
     for at in range(group):
         query_out[0, :, at * head_dim : (at + 1) * head_dim] = back[at * text_rows : (at + 1) * text_rows]
 
-
-def attention(tiles, queries, out_grad, keys, values, gain):
+    @pl.when(turn == pl.num_programs(0) * heads - 1)
+    def _():
+        for copy in exchange(sizes, groups, vision, columns_out, *sems)[1]:
+            copy.wait()
+
+
+def attention(sizes, tiles, queries, out_grad, keys, values, gain, vision):
+    pairs, n, heads_cut = sizes
+    rows, width = vision.shape[1:]
     samples, text_rows, query_width = queries.shape
     tokens, key_width = keys.shape[1:]
     head_dim = gain.shape[1]
@@ -571,10 +578,15 @@
     tall = pl.BlockSpec((1, tokens, head_dim), lambda s, h: (s, 0, h))
     flops = samples * query_width * text_rows * tokens * 10
     part = jax.ShapeDtypeStruct((samples, tokens, key_width), BF16)
+    groups = samples if heads_cut % samples == 0 else 1
+    each = 1 if groups > 1 else samples
+    chunks = chunks_of(width, pairs, n)
+    cut = jax.ShapeDtypeStruct((chunks, pairs, each, n, rows, width // (pairs * chunks * n)), BF16)
+    dma = pltpu.SemaphoreType.DMA
     return pl.pallas_call(
-        functools.partial(attention_kernel, group, tokens // MAX_TILES),
+        functools.partial(attention_kernel, sizes, groups, group, tokens // MAX_TILES),
         grid=(samples, heads),
-        out_shape=(jax.ShapeDtypeStruct(queries.shape, BF16), part, part),
+        out_shape=(jax.ShapeDtypeStruct(queries.shape, BF16), part, part, cut),
         in_specs=[
             pl.BlockSpec(memory_space=pltpu.SMEM),
             wide,
@@ -582,34 +594,46 @@
             tall,
             tall,
             pl.BlockSpec((1, head_dim), lambda s, h: (0, 0)),
+            pl.BlockSpec(memory_space=pltpu.HBM),
         ],
-        out_specs=(wide, tall, tall),
-        compiler_params=pltpu.CompilerParams(vmem_limit_bytes=48 * 1024 * 1024),
+        out_specs=(wide, tall, tall, pl.BlockSpec(memory_space=pltpu.HBM)),
+        scratch_shapes=[
+            dma((chunks, each, pairs * n)),
+            dma((chunks, each, pairs * n)),
+            dma((chunks, each)),
+        ],
+        compiler_params=pltpu.CompilerParams(
+            collective_id=5, has_side_effects=True, vmem_limit_bytes=40 * 1024 * 1024
+        ),
         cost_estimate=pl.CostEstimate(flops=flops, bytes_accessed=8_000_000, transcendentals=0),
         name="attention",
-    )(tiles, queries, out_grad, keys, values, gain)
+    )(tiles, queries, out_grad, keys, values, gain, vision)
 
 
 def local(sizes, queries, vision, key_weight, value_weight, query_gain, key_gain, out_grad, tile_count):
     pairs, n, heads_cut = sizes
     samples, rows, model_width = vision.shape
     columns = key_weight.shape[1]
-    keys_all, values_all, key_raw, column_vision = project(
+    keys_all, values_all, key_raw = project(
         sizes, vision, key_weight, value_weight, key_gain[None]
     )
-    query_grad, key_part, value_part = attention(
+    query_grad, key_part, value_part, half = attention(
+        sizes,
         tile_count,
         queries,
         out_grad,
         keys_all.reshape(samples, n * rows, columns),
         values_all.reshape(samples, n * rows, columns),
         query_gain[None],
-    )
-    key_grad, value_grad = ring_scatter(
+        vision,
+    )
+    key_grad, value_grad, column_vision = ring_scatter(
+        sizes,
         key_part.reshape(samples, n, rows, columns),
         value_part.reshape(samples, n, rows, columns),
         key_raw,
         key_gain[None],
+        half,
         2,
     )
     every_key, every_value, vision_grad = vision_gather(

time: 201 us -> 192 us (0.955)
  Pallas kernels: 178 us -> 171 us
  local copies, waits for them, and re-layouts: 10.2 us -> 7.65 us
    pallas_call x3, Pallas kernels: 100 us -> 93.9 us  [the longest x1 40 us: project(): pl.pallas_call(functools.partial(project_kernel, sizes), out_shape=(gathe...]
    unnamed x27 -> x26, local copies, waits for them, and re-layouts: 10.2 us -> 7.65 us
where the time goes in v3:
time: 192 us
  Pallas kernels  171 us (89%)
  other arithmetic  10.8 us (6%)
  local copies, waits for them, and re-layouts  7.65 us (4%)
    pallas_call x1, Pallas kernels, ring_gather(): pl.pallas_call(functools.partial(gather_kernel, n, pairs), out_shape=(out...  44.7 us
    pallas_call x1, Pallas kernels, project(): pl.pallas_call(functools.partial(project_kernel, sizes), out_shape=(gathe...  40 us
    pallas_call x1, Pallas kernels, vision_gather(): pl.pallas_call(functools.partial(vision_kernel, sizes, tile), out_shape=(...  32.6 us
    pallas_call x1, Pallas kernels, ring_scatter(): pl.pallas_call(functools.partial(scatter_kernel, n, groups, gain.shape[1]...  32 us
    pallas_call x1, Pallas kernels, attention(): pl.pallas_call(functools.partial(attention_kernel, sizes, groups, group,...  21.9 us
    convert_element_type x1, other arithmetic, local(): value_rows.reshape(model_width, columns).astype(F32)  10.8 us
    unnamed x26, local copies, waits for them, and re-layouts  7.65 us

profile of v3, /device:TPU:0, one launch (start us, length us, event | category | flops | bytes accessed | tf_op | source)
XLA Modules:
  0.0 192.1 jit_solution(4409471020155956475)
XLA Ops:
  0.6 0.0 copy-start.3
  0.6 0.0 copy-start.4
  0.7 0.0 copy-start.6
  0.7 0.0 copy-start.7
  0.7 40.0 %project_gather.1 = (bf16[2,8,80,512]{3,2,1,0:T(8,128)(2,1)}, bf16[2,8,80,512]{3,2,1,0:T(8,128)(2,1)}, f32[2,80,512]{2,1,0:T(8,128)}) custom-call(bf16[2,80,4096]{2,1,0:T(8,128)(2,1)} %vision.1, bf16[4096,512]{1,0:T(8,128)(2,1)} %key_hbm.3, bf16[4096,512]{1,0:T(8,128)(2,1)} %value_hbm.3, f32[1,128]{1,0:T(1,128)} %bitcast.55), custom_call_target="tpu_custom_call" | custom-call | flops 24999999488 | bytes 2293760 | tf_op jit(solution)/shard_map/project_gather/pallas_call | solution.py:238
  40.7 0.0 copy-done.3
  40.7 0.0 copy-done.4
  40.7 0.0 copy-done.6
  40.7 0.0 copy-done.7
  40.7 0.0 copy-start.5
  40.7 1.2 copy-done.5
  41.9 1.3 copy-done.9
  43.2 0.0 copy-start.10
  43.2 1.3 copy-done.10
  44.6 0.0 copy-start.8
  44.6 21.9 %attention.1 = (bf16[2,128,2048]{2,1,0:T(8,128)(2,1)S(1)}, bf16[2,640,512]{2,1,0:T(8,128)(2,1)S(1)}, bf16[2,640,512]{2,1,0:T(8,128)(2,1)S(1)}, bf16[2,2,1,8,80,128]{5,4,3,2,1,0:T(8,128)(2,1)S(1)}) custom-call(s32[2]{0:T(128)S(1)} %copy-done.6, bf16[2,128,2048]{2,1,0:T(8,128)(2,1)S(1)} %copy-done.4, bf16[2,128,2048]{2,1,0:T(8,128)(2,1)S(1)} %copy-done.5, ...), custom_call_target="tpu_custom_call" | custom-call | flops 3355443200 | bytes 8000000 | tf_op jit(solution)/shard_map/attention/pallas_call | solution.py:586
  66.5 0.0 copy-done.8
  66.5 0.0 copy-done.11
  66.5 0.0 copy-start.1
  66.5 0.0 copy-start.2
  66.5 32.0 %ring_scatter.1 = (bf16[2,80,512]{2,1,0:T(8,128)(2,1)S(1)}, bf16[2,80,512]{2,1,0:T(8,128)(2,1)S(1)}, bf16[2,2,2,8,80,128]{5,4,3,2,1,0:T(8,128)(2,1)S(1)}) custom-call(bf16[2,8,80,512]{3,2,1,0:T(8,128)(2,1)S(1)} %bitcast.57, bf16[2,8,80,512]{3,2,1,0:T(8,128)(2,1)S(1)} %bitcast.58, f32[2,80,512]{2,1,0:T(8,128)S(1)} %copy-done.11, f32[1,128]{1,0:T(1,128)S(1)} %bitcast.56, ...), custom_call_target="tpu_custom_call" | custom-call | flops 24999999488 | bytes 2293760 | tf_op jit(solution)/shard_map/ring_scatter/pallas_call | solution.py:460
  98.5 0.0 copy-done.1
  98.5 0.0 copy-done.2
  98.5 32.6 %vision_gather.1 = (bf16[2,2,8,80,512]{4,3,2,1,0:T(8,128)(2,1)S(1)}, bf16[2,2,8,80,512]{4,3,2,1,0:T(8,128)(2,1)S(1)}, bf16[160,2048]{1,0:T(8,128)(2,1)S(1)}) custom-call(bf16[2,80,512]{2,1,0:T(8,128)(2,1)S(1)} %get-tuple-element.26.key_ref, bf16[2,80,512]{2,1,0:T(8,128)(2,1)S(1)} %get-tuple-element.27.value_ref, bf16[4096,512]{1,0:T(8,128)(2,1)S(1)} %copy-done.1, ...), custom_call_target="tpu_custom_call" | custom-call | flops 24999999488 | bytes 2293760 | tf_op jit(solution)/shard_map/vision_gather/pallas_call | solution.py:345
  131.2 0.9 fusion.13.first_ref
  132.0 0.9 fusion.10.second_ref
  132.9 44.7 %ring_gather_4.1 = (bf16[2,2,8,128,512]{4,3,2,1,0:T(8,128)(2,1)S(1)}, bf16[2,2,8,128,512]{4,3,2,1,0:T(8,128)(2,1)S(1)}) custom-call(bf16[2,128,512]{2,1,0:T(8,128)(2,1)S(1)} %fusion.13.first_ref, bf16[2,128,512]{2,1,0:T(8,128)(2,1)S(1)} %fusion.10.second_ref), custom_call_target="tpu_custom_call" | custom-call | flops 24999999488 | bytes 3670016 | tf_op jit(solution)/shard_map/ring_gather_4/pallas_call | solution.py:161
  177.6 0.0 copy-start
  177.6 2.0 %copy-done = bf16[2,2,8,128,512]{4,3,2,1,0:T(8,128)(2,1)} copy-done((bf16[2,2,8,128,512]{4,3,2,1,0:T(8,128)(2,1)}, bf16[2,2,8,128,512]{4,3,2,1,0:T(8,128)(2,1)S(1)}, u32[]{:S(2)}) %copy-start) | copy-done | bytes 4194328
  179.6 10.8 %bitcast_convert_fusion = (f32[4096,512]{1,0:T(8,128)}, f32[4096,512]{1,0:T(8,128)}) fusion(bf16[2,2,8,128,512]{4,3,2,1,0:T(8,128)(2,1)} %copy-done, bf16[2,2,8,128,512]{4,3,2,1,0:T(8,128)(2,1)S(1)} %get-tuple-element.32), kind=kLoop, calls=%fused_computation | loop fusion | flops 4194304 | bytes 25165824 | tf_op jit(solution)/shard_map/convert_element_type | solution.py:655
  190.3 1.0 copy.19
  191.3 0.8 copy.20
  (2 shorter events, 0.0 us)
Async XLA Ops:
  0.6 40.0 %copy-start.3 = (bf16[2,80,4096]{2,1,0:T(8,128)(2,1)S(1)}, bf16[2,80,4096]{2,1,0:T(8,128)(2,1)}, u32[]{:S(2)}) copy-start(bf16[2,80,4096]{2,1,0:T(8,128)(2,1)} %vision.1) | copy-start | bytes 3932164
  0.6 40.0 %copy-start.4 = (bf16[2,128,2048]{2,1,0:T(8,128)(2,1)S(1)}, bf16[2,128,2048]{2,1,0:T(8,128)(2,1)}, u32[]{:S(2)}) copy-start(bf16[2,128,2048]{2,1,0:T(8,128)(2,1)} %query_ref.1) | copy-start | bytes 3145732
  0.7 40.0 %copy-start.6 = (s32[2]{0:T(128)S(1)}, s32[2]{0:T(128)}, u32[]{:S(2)}) copy-start(s32[2]{0:T(128)} %tiles_ref.1) | copy-start | bytes 28
  0.7 40.0 %copy-start.7 = (f32[128]{0:T(128)S(1)}, f32[128]{0:T(128)}, u32[]{:S(2)}) copy-start(f32[128]{0:T(128)} %param.12) | copy-start | bytes 1540
  40.7 1.2 copy-start.5
  41.9 1.3 copy-start.9
  43.2 1.3 copy-start.10
  44.6 21.9 %copy-start.8 = (f32[128]{0:T(128)S(1)}, f32[128]{0:T(128)}, u32[]{:S(2)}) copy-start(f32[128]{0:T(128)} %param.13) | copy-start | bytes 1540
  44.6 22.0 %copy-start.11 = (f32[2,80,512]{2,1,0:T(8,128)S(1)}, f32[2,80,512]{2,1,0:T(8,128)}, u32[]{:S(2)}) copy-start(f32[2,80,512]{2,1,0:T(8,128)} %get-tuple-element.24.raw_ref) | copy-start | bytes 983044
  66.5 32.0 %copy-start.1 = (bf16[4096,512]{1,0:T(8,128)(2,1)S(1)}, bf16[4096,512]{1,0:T(8,128)(2,1)}, u32[]{:S(2)}) copy-start(bf16[4096,512]{1,0:T(8,128)(2,1)} %key_hbm.3) | copy-start | bytes 12582916
  66.5 32.0 %copy-start.2 = (bf16[4096,512]{1,0:T(8,128)(2,1)S(1)}, bf16[4096,512]{1,0:T(8,128)(2,1)}, u32[]{:S(2)}) copy-start(bf16[4096,512]{1,0:T(8,128)(2,1)} %value_hbm.3) | copy-start | bytes 12582916
  177.6 2.0 %copy-start = (bf16[2,2,8,128,512]{4,3,2,1,0:T(8,128)(2,1)}, bf16[2,2,8,128,512]{4,3,2,1,0:T(8,128)(2,1)S(1)}, u32[]{:S(2)}) copy-start(bf16[2,2,8,128,512]{4,3,2,1,0:T(8,128)(2,1)S(1)} %get-tuple-element.33) | copy-start | bytes 12582916
